TPU v7x, 256 devices: a whole 4x4x8 slice. The times are simulated.
256 devices in a mesh: row: 16 (over y_hi, x, core), col: 16 (over z, y_lo).
Axes of the slice: x: 4, y: 4 (y_hi: 2, y_lo: 2; y = y_hi * 2 + y_lo), z: 8, core: 2. Of those that a mesh axis runs over, the one named last changes fastest.
Arguments:
- features: bfloat16 [32768, 512], P(('row', 'col')), may hold values from -6 to 6
- coefs: bfloat16 [32768], P(('row', 'col')), may hold values from -150 to 150
Outputs:
- grads: bfloat16 [32768, 512], P(('row', 'col'))
- recolored: bfloat16 [32768, 512], P(('row', 'col'))
All inputs are finite; a program needn't handle non-finite values.
Results may differ from a plain program's by a relative error of at most 0.0025.
The roundings to bfloat16 on the way count: a program that leaves them out, or rounds other values in their place, can miss the bound.
Values may be sent and summed in bfloat16 or wider, within the bound.
No kernel may reach another device: no remote copies, remote signals or barrier semaphores. Data moves between devices by JAX's collectives and lax.ppermute only.
A program may use at most 64 MiB of HBM per device.

v0:
```python
import math

import jax
import jax.numpy as jnp
from jax import lax
from jax.experimental import pallas as pl
from jax.experimental.pallas import tpu as pltpu
from jax.sharding import Mesh, PartitionSpec as P


AXES = ("yh", "x", "c", "z", "yl")
SIZES = (2, 4, 2, 8, 2)
EXTRA = 8
LANES = 128
VMEM_LIMIT = 12 * 2**20
F32, BF16 = jnp.float32, jnp.bfloat16


def swapped(value, axis):
    return lax.ppermute(value, axis, [(0, 1), (1, 0)])


def from_everyone(value, axes):
    copies = jnp.broadcast_to(value, (lax.axis_size(axes), *value.shape))
    return lax.all_to_all(copies, axes, split_axis=0, concat_axis=0, tiled=True)


def along_z(value):
    count = lax.axis_size("z")
    pairs = [(z, (z + 1) % count) for z in range(count)]
    pairs += [(count + z, count + (z - 1) % count) for z in range(count)]
    return lax.ppermute(value, ("c", "z"), pairs)


def extra_rows(features, coefs):
    full = features.astype(F32)
    norms = jnp.sum(full * full, axis=1)
    high = lax.reduce_precision(norms, 8, 7)
    middle = lax.reduce_precision(norms - high, 8, 7)
    low = lax.reduce_precision(norms - high - middle, 8, 7)
    rows = jnp.stack([coefs.astype(F32), high, middle, low]).astype(BF16)
    return jnp.pad(rows, ((0, EXTRA - 4), (0, 0)))


def widened(rows, width):
    return jnp.pad(rows, ((0, 0), (0, width - rows.shape[1])))


def pair_block(features, coefs):
    points, width = features.shape
    extras = extra_rows(features, coefs)
    block = jnp.concatenate([features, widened(extras, width)])
    other = swapped(block, "yh")
    extras = jnp.concatenate([extras, other[points:, :points]], axis=1)
    return jnp.concatenate([features, other[:points], widened(extras, width)])


def tile_kernel(first, last, row_refs_count, chunk_count, *refs):
    row_refs, refs = refs[:row_refs_count], refs[row_refs_count:]
    chunk_refs, refs = refs[:chunk_count], refs[chunk_count:]
    if not first:
        old_ref, old_totals_ref, *refs = refs
    out_ref, refs = refs[0], refs[1:]
    if not last:
        totals_ref, refs = refs[0], refs[1:]
    (weighted_ref,) = refs
    row_count, width = row_refs[0].shape
    points = chunk_refs[0].shape[0] - EXTRA
    scale = 2.0 / width * math.log2(math.e)
    lane = lax.broadcasted_iota(jnp.int32, (LANES, LANES), 1)
    sublane = lax.broadcasted_iota(jnp.int32, (LANES, LANES), 0)
    for at, ref in enumerate(chunk_refs):
        for k in range(0, points, LANES):
            coef_row = ref[points : points + 1, k : k + LANES].astype(F32)
            spread = jnp.where(lane == sublane, coef_row, 0.0).astype(BF16)
            weighted_ref[at * points + k : at * points + k + LANES, :] = jnp.dot(
                spread, ref[k : k + LANES, :], preferred_element_type=F32
            ).astype(BF16)

    for s in range(0, row_refs_count, 2):
        strip = 2 * row_count
        here = slice(s * row_count, s * row_count + strip)
        rows = jnp.concatenate([row_refs[s][...], row_refs[s + 1][...]])
        full = rows.astype(F32)
        row_terms = jnp.sum(full * full, axis=1, keepdims=True) * (-scale)
        totals = jnp.zeros((strip, LANES), F32) if first else old_totals_ref[here, :]
        kernels = []
        for ref in chunk_refs:
            extra = ref[points : points + EXTRA, :points].astype(F32)
            col_terms = (extra[1:2] + extra[2:3] + extra[3:4]) * (-scale)
            products = lax.dot_general(
                rows, ref[:points, :], (((1,), (1,)), ((), ())), preferred_element_type=F32
            )
            kernel = jnp.exp2(products * (2.0 * scale) + (row_terms + col_terms)).astype(BF16)
            terms = kernel.astype(F32) * extra[0:1]
            for k in range(0, points, LANES):
                totals = totals + terms[:, k : k + LANES]
            kernels.append(kernel)
        moments = jnp.dot(
            jnp.concatenate(kernels, axis=1), weighted_ref[...], preferred_element_type=F32
        )
        if not first:
            moments = moments + old_ref[here, :]
        if last:
            moments = moments - jnp.sum(totals, axis=1, keepdims=True) * full
            x_at, yl_at = lax.axis_index("x"), lax.axis_index("yl")
            for k in range(0, strip, LANES):
                away, beside = divmod((here.start + k) // LANES, 2)
                place = 2 * lax.rem(x_at + away, row_refs_count) + lax.rem(yl_at + beside, 2)
                out_ref[place] = moments[k : k + LANES]
        else:
            out_ref[here, :] = moments
            totals_ref[here, :] = totals


def add_tiles(rows, chunks, carried, last):
    row_count, width = sum(r.shape[0] for r in rows), rows[0].shape[1]
    columns = sum(chunk.shape[0] - EXTRA for chunk in chunks)
    first = carried is None
    spec = pl.BlockSpec(memory_space=pltpu.VMEM)
    operands = [*rows, *chunks] + ([] if first else list(carried))
    aliases = {}
    if last:
        out_shape = [jax.ShapeDtypeStruct((row_count // LANES, LANES, width), F32)]
    else:
        out_shape = [
            jax.ShapeDtypeStruct((row_count, width), F32),
            jax.ShapeDtypeStruct((row_count, LANES), F32),
        ]
        if not first:
            aliases = {len(operands) - 2: 0, len(operands) - 1: 1}

    def body(*refs):
        tile_kernel(first, last, len(rows), len(chunks), *refs)

    return pl.pallas_call(
        body,
        out_shape=out_shape,
        in_specs=[spec] * len(operands),
        out_specs=[spec] * len(out_shape),
        scratch_shapes=[pltpu.VMEM((columns, width), BF16)],
        input_output_aliases=aliases,
        compiler_params=pltpu.CompilerParams(vmem_limit_bytes=VMEM_LIMIT),
        cost_estimate=pl.CostEstimate(
            flops=4 * row_count * columns * width,
            bytes_accessed=4 * row_count * width,
            transcendentals=row_count * columns,
        ),
    )(*operands)


def step(features, coefs):
    points, width = features.shape
    gamma = 2.0 / width
    row_axes = ("x", "yl")
    chip_axes = ("yh", "x", "z", "yl")

    beside = swapped(features, "yl")
    rows = [jnp.concatenate([features, beside])]
    x_count = lax.axis_size("x")
    for shift in range(1, x_count):
        pairs = [(x, (x - shift) % x_count) for x in range(x_count)]
        rows.append(lax.ppermute(rows[0], "x", pairs))
    near = pair_block(features, coefs)
    far = swapped(near, "c")
    groups = [[near, far]]
    hops = lax.axis_size("z") // 2
    for hop in range(1, hops + 1):
        near = along_z(near)
        other_near = swapped(near, "c")
        if hop == hops:
            groups += [[near], [other_near]]
            break
        far = along_z(far)
        other_far = swapped(far, "c")
        groups.append([near, far, other_near, other_far])

    carried = None
    for at, group in enumerate(groups):
        carried = add_tiles(rows, group, carried, at == len(groups) - 1)
    (partial,) = carried
    summed = jnp.sum(lax.all_to_all(partial, row_axes, 0, 0, tiled=True), axis=0)
    grads = (2.0 * gamma * summed).astype(BF16)

    core = lax.axis_index("c")
    half = width // 2
    both = jnp.concatenate([grads, swapped(grads, "c")])
    own_half = jnp.where(core == 0, both[:, :half], both[:, half:])
    gram = jnp.einsum("pa,pb->ab", own_half, both, preferred_element_type=F32)
    chips = lax.axis_size(chip_axes)
    parts = lax.all_to_all(gram.reshape(chips, -1, 128), chip_axes, 0, 0, tiled=True)
    point_count = points * chips * lax.axis_size("c")
    own_agop = (jnp.sum(parts, axis=0) / point_count).astype(BF16)
    own_rows = from_everyone(own_agop, chip_axes).reshape(half, width)
    other_rows = swapped(own_rows, "c")
    upper = jnp.where(core == 0, own_rows, other_rows)
    lower = jnp.where(core == 0, other_rows, own_rows)
    agop = jnp.concatenate([upper, lower])
    recolored = jnp.dot(features, agop, preferred_element_type=F32)
    return grads, recolored.astype(BF16)


def solution(mesh):
    fine = Mesh(mesh.devices.reshape(SIZES), AXES)
    return jax.shard_map(
        step,
        mesh=fine,
        in_specs=(P(AXES, None), P(AXES)),
        out_specs=(P(AXES, None), P(AXES, None)),
        check_vma=False,
    )
```

profile of v0, /device:TPU:2, one launch (start us, length us, event | category | flops | bytes accessed | tf_op | source)
XLA Modules:
  0.0 147.3 jit_solution(17266484559442157739)
XLA Ops:
  0.6 1.0 multiply_reduce_fusion
  1.7 0.7 fusion.22
  2.3 0.9 fusion.6
  3.2 3.3 %collective-permute-start.4 = (bf16[136,512]{1,0:T(8,128)(2,1)S(1)}, bf16[136,512]{1,0:T(8,128)(2,1)S(1)}, u32[]{:S(2)}, u32[]{:S(2)}) collective-permute-start(bf16[136,512]{1,0:T(8,128)(2,1)S(1)} %fusion.6), channel_id=1, source_target_pairs={{0,128},{128,0},{1,129},{129,1},{2,130},{130,2},{3,131},{131,3},{4... | collective-permute-start | bytes 417800 | tf_op jit(solution)/shard_map/ppermute | solution.py:20
  6.5 3.7 %collective-permute-done.4 = bf16[136,512]{1,0:T(8,128)(2,1)S(1)} collective-permute-done((bf16[136,512]{1,0:T(8,128)(2,1)S(1)}, bf16[136,512]{1,0:T(8,128)(2,1)S(1)}, u32[]{:S(2)}, u32[]{:S(2)}) %collective-permute-start.4) | collective-permute-done | bytes 139296 | tf_op jit(solution)/shard_map/ppermute | solution.py:20
  10.3 0.9 pad_maximum_fusion.1.refs_4_
  11.2 0.1 collective-permute-start.10
  11.3 2.0 %collective-permute-start.5 = (bf16[264,512]{1,0:T(8,128)(2,1)S(1)}, bf16[264,512]{1,0:T(8,128)(2,1)S(1)}, u32[]{:S(2)}, u32[]{:S(2)}) collective-permute-start(bf16[264,512]{1,0:T(8,128)(2,1)S(1)} %pad_maximum_fusion.1.refs_4_), channel_id=1, source_target_pairs={{0,2},{2,4},{4,6},{6,8},{8,10},{10,12},{12,14},{14,0},{16,30},{18,... | collective-permute-start | bytes 811016 | tf_op jit(solution)/shard_map/ppermute | solution.py:32
  13.3 1.6 %collective-permute-start = (bf16[128,512]{1,0:T(8,128)(2,1)}, bf16[128,512]{1,0:T(8,128)(2,1)S(1)}, u32[]{:S(2)}, u32[]{:S(2)}) collective-permute-start(bf16[128,512]{1,0:T(8,128)(2,1)} %param.2), channel_id=1, source_target_pairs={{0,1},{1,0},{2,3},{3,2},{4,5},{5,4},{6,7},{7,6},{8,9},{9,8},{10,11... | collective-permute-start | bytes 393224 | tf_op jit(solution)/shard_map/ppermute | solution.py:20
  14.9 0.0 collective-permute-done.10.refs_5_
  14.9 1.9 %collective-permute-start.11 = (bf16[264,512]{1,0:T(8,128)(2,1)S(1)}, bf16[264,512]{1,0:T(8,128)(2,1)S(1)}, u32[]{:S(2)}, u32[]{:S(2)}) collective-permute-start(bf16[264,512]{1,0:T(8,128)(2,1)S(1)} %collective-permute-done.10.refs_5_), channel_id=1, source_target_pairs={{0,2},{2,4},{4,6},{6,8},{8,10},{10,12},{12,14},{14,0},{16,30},{18,... | collective-permute-start | bytes 811016 | tf_op jit(solution)/shard_map/ppermute | solution.py:32
  16.8 0.9 constant_dynamic-update-slice_fusion.1
  17.7 4.0 %collective-permute-done.5.refs_4_ = bf16[264,512]{1,0:T(8,128)(2,1)S(1)} collective-permute-done((bf16[264,512]{1,0:T(8,128)(2,1)S(1)}, bf16[264,512]{1,0:T(8,128)(2,1)S(1)}, u32[]{:S(2)}, u32[]{:S(2)}) %collective-permute-start.5) | collective-permute-done | bytes 270368 | tf_op jit(solution)/shard_map/ppermute | solution.py:32
  21.7 0.0 collective-permute-start.6
  21.7 0.0 collective-permute-done
  21.7 0.6 collective-permute-start.1
  22.3 2.3 %collective-permute-done.11.refs_5_ = bf16[264,512]{1,0:T(8,128)(2,1)S(1)} collective-permute-done((bf16[264,512]{1,0:T(8,128)(2,1)S(1)}, bf16[264,512]{1,0:T(8,128)(2,1)S(1)}, u32[]{:S(2)}, u32[]{:S(2)}) %collective-permute-start.11) | collective-permute-done | bytes 270368 | tf_op jit(solution)/shard_map/ppermute | solution.py:32
  24.6 0.0 collective-permute-start.12
  24.6 2.1 %collective-permute-start.2 = (bf16[256,512]{1,0:T(8,128)(2,1)S(1)}, bf16[256,512]{1,0:T(8,128)(2,1)S(1)}, u32[]{:S(2)}, u32[]{:S(2)}) collective-permute-start(bf16[256,512]{1,0:T(8,128)(2,1)S(1)} %constant_dynamic-update-slice_fusion.refs_0_), channel_id=1, source_target_pairs={{0,64},{32,96},{64,0},{96,32},{1,65},{33,97},{65,1},{97,33},{2,66}... | collective-permute-start | bytes 786440 | tf_op jit(solution)/shard_map/ppermute | solution.py:163
  26.7 1.9 %collective-permute-start.18 = (bf16[264,512]{1,0:T(8,128)(2,1)S(1)}, bf16[264,512]{1,0:T(8,128)(2,1)S(1)}, u32[]{:S(2)}, u32[]{:S(2)}) collective-permute-start(bf16[264,512]{1,0:T(8,128)(2,1)S(1)} %collective-permute-done.5.refs_4_), channel_id=1, source_target_pairs={{0,16},{16,0},{1,17},{17,1},{2,18},{18,2},{3,19},{19,3},{4,20},{20... | collective-permute-start | bytes 811016 | tf_op jit(solution)/shard_map/ppermute | solution.py:20
  28.6 0.7 collective-permute-done.6.refs_4_
  29.3 0.0 collective-permute-start.7
  29.3 0.4 collective-permute-done.1.refs_1_
  29.7 1.5 %collective-permute-start.3 = (bf16[256,512]{1,0:T(8,128)(2,1)S(1)}, bf16[256,512]{1,0:T(8,128)(2,1)S(1)}, u32[]{:S(2)}, u32[]{:S(2)}) collective-permute-start(bf16[256,512]{1,0:T(8,128)(2,1)S(1)} %constant_dynamic-update-slice_fusion.refs_0_), channel_id=1, source_target_pairs={{0,32},{32,64},{64,96},{96,0},{1,33},{33,65},{65,97},{97,1},{2,34}... | collective-permute-start | bytes 786440 | tf_op jit(solution)/shard_map/ppermute | solution.py:163
  31.2 5.1 %collective-permute-done.2.refs_2_ = bf16[256,512]{1,0:T(8,128)(2,1)S(1)} collective-permute-done((bf16[256,512]{1,0:T(8,128)(2,1)S(1)}, bf16[256,512]{1,0:T(8,128)(2,1)S(1)}, u32[]{:S(2)}, u32[]{:S(2)}) %collective-permute-start.2) | collective-permute-done | bytes 262176 | tf_op jit(solution)/shard_map/ppermute | solution.py:163
  36.2 1.1 collective-permute-start.19
  37.3 0.0 collective-permute-done.12.refs_5_
  37.3 0.1 collective-permute-start.13
  37.4 2.1 %collective-permute-done.3.refs_3_ = bf16[256,512]{1,0:T(8,128)(2,1)S(1)} collective-permute-done((bf16[256,512]{1,0:T(8,128)(2,1)S(1)}, bf16[256,512]{1,0:T(8,128)(2,1)S(1)}, u32[]{:S(2)}, u32[]{:S(2)}) %collective-permute-start.3) | collective-permute-done | bytes 262176 | tf_op jit(solution)/shard_map/ppermute | solution.py:163
  39.4 1.5 %collective-permute-start.16 = (bf16[264,512]{1,0:T(8,128)(2,1)S(1)}, bf16[264,512]{1,0:T(8,128)(2,1)S(1)}, u32[]{:S(2)}, u32[]{:S(2)}) collective-permute-start(bf16[264,512]{1,0:T(8,128)(2,1)S(1)} %collective-permute-done.6.refs_4_), channel_id=1, source_target_pairs={{0,16},{16,0},{1,17},{17,1},{2,18},{18,2},{3,19},{19,3},{4,20},{20... | collective-permute-start | bytes 811016 | tf_op jit(solution)/shard_map/ppermute | solution.py:20
  41.0 0.0 collective-permute-done.18.refs_6_
  41.0 0.0 collective-permute-start.17
  41.0 0.0 collective-permute-done.7.refs_4_
  41.0 1.2 collective-permute-start.8
  42.2 1.5 %shard_map.41 = (f32[1024,512]{1,0:T(8,128)S(1)}, f32[1024,128]{1,0:T(8,128)S(1)}) custom-call(bf16[256,512]{1,0:T(8,128)(2,1)S(1)} %constant_dynamic-update-slice_fusion.refs_0_, bf16[256,512]{1,0:T(8,128)(2,1)S(1)} %collective-permute-done.1.refs_1_, bf16[256,512]{1,0:T(8,128)(2,1)S(1)} %collective-permute-done.2.refs_2_, ...), custom_call_target="tpu_custom_call" | custom-call | flops 1073741824 | bytes 2097152 | tf_op jit(solution)/shard_map/pallas_call | solution.py:136
  43.7 0.0 collective-permute-done.19.refs_7_
  43.7 1.7 %collective-permute-start.14 = (bf16[264,512]{1,0:T(8,128)(2,1)S(1)}, bf16[264,512]{1,0:T(8,128)(2,1)S(1)}, u32[]{:S(2)}, u32[]{:S(2)}) collective-permute-start(bf16[264,512]{1,0:T(8,128)(2,1)S(1)} %collective-permute-done.7.refs_4_), channel_id=1, source_target_pairs={{0,16},{16,0},{1,17},{17,1},{2,18},{18,2},{3,19},{19,3},{4,20},{20... | collective-permute-start | bytes 811016 | tf_op jit(solution)/shard_map/ppermute | solution.py:20
  45.4 0.0 collective-permute-done.13.refs_5_
  45.4 0.1 collective-permute-start.15
  45.6 3.0 %shard_map.42 = (f32[1024,512]{1,0:T(8,128)S(1)}, f32[1024,128]{1,0:T(8,128)S(1)}) custom-call(bf16[256,512]{1,0:T(8,128)(2,1)S(1)} %constant_dynamic-update-slice_fusion.refs_0_, bf16[256,512]{1,0:T(8,128)(2,1)S(1)} %collective-permute-done.1.refs_1_, ...), custom_call_target="tpu_custom_call", output_to_operand_aliasing={{0}: (8, {}), {1}: (9, {})} | custom-call | flops 2147483648 | bytes 2097152 | tf_op jit(solution)/shard_map/pallas_call | solution.py:136
  48.5 0.4 collective-permute-done.8.refs_4_
  48.9 0.1 collective-permute-start.9
  49.0 0.0 collective-permute-done.16.refs_6_
  49.0 0.0 collective-permute-done.17.refs_7_
  49.0 2.9 %shard_map.43 = (f32[1024,512]{1,0:T(8,128)S(1)}, f32[1024,128]{1,0:T(8,128)S(1)}) custom-call(bf16[256,512]{1,0:T(8,128)(2,1)S(1)} %constant_dynamic-update-slice_fusion.refs_0_, bf16[256,512]{1,0:T(8,128)(2,1)S(1)} %collective-permute-done.1.refs_1_, ...), custom_call_target="tpu_custom_call", output_to_operand_aliasing={{0}: (8, {}), {1}: (9, {})} | custom-call | flops 2147483648 | bytes 2097152 | tf_op jit(solution)/shard_map/pallas_call | solution.py:136
  52.0 3.0 %shard_map.44 = (f32[1024,512]{1,0:T(8,128)S(1)}, f32[1024,128]{1,0:T(8,128)S(1)}) custom-call(bf16[256,512]{1,0:T(8,128)(2,1)S(1)} %constant_dynamic-update-slice_fusion.refs_0_, bf16[256,512]{1,0:T(8,128)(2,1)S(1)} %collective-permute-done.1.refs_1_, ...), custom_call_target="tpu_custom_call", output_to_operand_aliasing={{0}: (8, {}), {1}: (9, {})} | custom-call | flops 2147483648 | bytes 2097152 | tf_op jit(solution)/shard_map/pallas_call | solution.py:136
  55.0 1.5 %shard_map.45 = (f32[1024,512]{1,0:T(8,128)S(1)}, f32[1024,128]{1,0:T(8,128)S(1)}) custom-call(bf16[256,512]{1,0:T(8,128)(2,1)S(1)} %constant_dynamic-update-slice_fusion.refs_0_, bf16[256,512]{1,0:T(8,128)(2,1)S(1)} %collective-permute-done.1.refs_1_, ...), custom_call_target="tpu_custom_call", output_to_operand_aliasing={{0}: (5, {}), {1}: (6, {})} | custom-call | flops 536870912 | bytes 2097152 | tf_op jit(solution)/shard_map/pallas_call | solution.py:136
  56.5 0.0 collective-permute-done.9.refs_4_
  56.5 1.4 shard_map.46
  57.9 33.5 %all_to_all.15 = f32[8,128,512]{2,1,0:T(8,128)S(1)} all-to-all(f32[8,128,512]{2,1,0:T(8,128)S(1)} %shard_map.46), channel_id=1, replica_groups=mesh['yh'=2,'x'=4,'c'=2,'z'=8,'yl'=2] {'x','yl'}, dimensions={0} | all-to-all | bytes 4194304 | tf_op jit(solution)/shard_map/all_to_all | solution.py:182
  91.3 0.2 reduce_sum.31
  91.6 0.0 copy-start.1
  91.6 0.1 collective-permute-start.20
  91.7 1.3 collective-permute-done.20
  93.0 0.2 fusion.5
  93.3 0.0 copy-start
  93.4 30.1 %all_to_all.16 = f32[128,8,128]{2,1,0:T(8,128)S(1)} all-to-all(f32[128,8,128]{2,1,0:T(8,128)S(1)} %reshape.37), channel_id=1, replica_groups=mesh['yh'=2,'x'=4,'c'=2,'z'=8,'yl'=2] {'yh','x','z','yl'}, dimensions={0} | all-to-all | bytes 1048576 | tf_op jit(solution)/shard_map/all_to_all | solution.py:191
  123.5 0.1 reduce_sum.32
  123.7 20.7 %all_to_all.17 = bf16[128,8,128]{2,1,0:T(8,128)(2,1)S(1)} all-to-all(bf16[128,8,128]{2,1,0:T(8,128)(2,1)S(1)} %broadcast_in_dim.3), channel_id=1, replica_groups=mesh['yh'=2,'x'=4,'c'=2,'z'=8,'yl'=2] {'yh','x','z','yl'}, dimensions={0} | all-to-all | bytes 524288 | tf_op jit(solution)/shard_map/all_to_all | solution.py:25
  144.4 0.2 reshape.38
  144.5 0.1 collective-permute-start.21
  144.6 1.5 %collective-permute-done.21 = bf16[256,512]{1,0:T(8,128)(2,1)S(1)} collective-permute-done((bf16[256,512]{1,0:T(8,128)(2,1)S(1)}, bf16[256,512]{1,0:T(8,128)(2,1)S(1)}, u32[]{:S(2)}, u32[]{:S(2)}) %collective-permute-start.21) | collective-permute-done | bytes 262176 | tf_op jit(solution)/shard_map/ppermute | solution.py:20
  146.2 0.3 fusion
  146.6 0.8 copy.12
  (14 shorter events, 0.2 us)
Async XLA Ops:
  3.2 7.0 %collective-permute-start.4 = (bf16[136,512]{1,0:T(8,128)(2,1)S(1)}, bf16[136,512]{1,0:T(8,128)(2,1)S(1)}, u32[]{:S(2)}, u32[]{:S(2)}) collective-permute-start(bf16[136,512]{1,0:T(8,128)(2,1)S(1)} %fusion.6), channel_id=1, source_target_pairs={{0,128},{128,0},{1,129},{129,1},{2,130},{130,2},{3,131},{131,3},{4... | collective-permute-start | bytes 417800 | tf_op jit(solution)/shard_map/ppermute | solution.py:20
  11.2 3.7 %collective-permute-start.10 = (bf16[264,512]{1,0:T(8,128)(2,1)S(1)}, bf16[264,512]{1,0:T(8,128)(2,1)S(1)}, u32[]{:S(2)}, u32[]{:S(2)}) collective-permute-start(bf16[264,512]{1,0:T(8,128)(2,1)S(1)} %pad_maximum_fusion.1.refs_4_), channel_id=1, source_target_pairs={{0,16},{16,0},{1,17},{17,1},{2,18},{18,2},{3,19},{19,3},{4,20},{20... | collective-permute-start | bytes 811016 | tf_op jit(solution)/shard_map/ppermute | solution.py:20
  11.3 10.4 %collective-permute-start.5 = (bf16[264,512]{1,0:T(8,128)(2,1)S(1)}, bf16[264,512]{1,0:T(8,128)(2,1)S(1)}, u32[]{:S(2)}, u32[]{:S(2)}) collective-permute-start(bf16[264,512]{1,0:T(8,128)(2,1)S(1)} %pad_maximum_fusion.1.refs_4_), channel_id=1, source_target_pairs={{0,2},{2,4},{4,6},{6,8},{8,10},{10,12},{12,14},{14,0},{16,30},{18,... | collective-permute-start | bytes 811016 | tf_op jit(solution)/shard_map/ppermute | solution.py:32
  13.3 8.4 %collective-permute-start = (bf16[128,512]{1,0:T(8,128)(2,1)}, bf16[128,512]{1,0:T(8,128)(2,1)S(1)}, u32[]{:S(2)}, u32[]{:S(2)}) collective-permute-start(bf16[128,512]{1,0:T(8,128)(2,1)} %param.2), channel_id=1, source_target_pairs={{0,1},{1,0},{2,3},{3,2},{4,5},{5,4},{6,7},{7,6},{8,9},{9,8},{10,11... | collective-permute-start | bytes 393224 | tf_op jit(solution)/shard_map/ppermute | solution.py:20
  14.9 9.7 %collective-permute-start.11 = (bf16[264,512]{1,0:T(8,128)(2,1)S(1)}, bf16[264,512]{1,0:T(8,128)(2,1)S(1)}, u32[]{:S(2)}, u32[]{:S(2)}) collective-permute-start(bf16[264,512]{1,0:T(8,128)(2,1)S(1)} %collective-permute-done.10.refs_5_), channel_id=1, source_target_pairs={{0,2},{2,4},{4,6},{6,8},{8,10},{10,12},{12,14},{14,0},{16,30},{18,... | collective-permute-start | bytes 811016 | tf_op jit(solution)/shard_map/ppermute | solution.py:32
  21.7 7.7 %collective-permute-start.6 = (bf16[264,512]{1,0:T(8,128)(2,1)S(1)}, bf16[264,512]{1,0:T(8,128)(2,1)S(1)}, u32[]{:S(2)}, u32[]{:S(2)}) collective-permute-start(bf16[264,512]{1,0:T(8,128)(2,1)S(1)} %collective-permute-done.5.refs_4_), channel_id=1, source_target_pairs={{0,2},{2,4},{4,6},{6,8},{8,10},{10,12},{12,14},{14,0},{16,30},{18,... | collective-permute-start | bytes 811016 | tf_op jit(solution)/shard_map/ppermute | solution.py:32
  21.7 8.0 %collective-permute-start.1 = (bf16[256,512]{1,0:T(8,128)(2,1)S(1)}, bf16[256,512]{1,0:T(8,128)(2,1)S(1)}, u32[]{:S(2)}, u32[]{:S(2)}) collective-permute-start(bf16[256,512]{1,0:T(8,128)(2,1)S(1)} %constant_dynamic-update-slice_fusion.refs_0_), channel_id=1, source_target_pairs={{0,96},{32,0},{64,32},{96,64},{1,97},{33,1},{65,33},{97,65},{2,98}... | collective-permute-start | bytes 786440 | tf_op jit(solution)/shard_map/ppermute | solution.py:163
  24.6 12.8 %collective-permute-start.12 = (bf16[264,512]{1,0:T(8,128)(2,1)S(1)}, bf16[264,512]{1,0:T(8,128)(2,1)S(1)}, u32[]{:S(2)}, u32[]{:S(2)}) collective-permute-start(bf16[264,512]{1,0:T(8,128)(2,1)S(1)} %collective-permute-done.11.refs_5_), channel_id=1, source_target_pairs={{0,2},{2,4},{4,6},{6,8},{8,10},{10,12},{12,14},{14,0},{16,30},{18,... | collective-permute-start | bytes 811016 | tf_op jit(solution)/shard_map/ppermute | solution.py:32
  24.6 11.7 %collective-permute-start.2 = (bf16[256,512]{1,0:T(8,128)(2,1)S(1)}, bf16[256,512]{1,0:T(8,128)(2,1)S(1)}, u32[]{:S(2)}, u32[]{:S(2)}) collective-permute-start(bf16[256,512]{1,0:T(8,128)(2,1)S(1)} %constant_dynamic-update-slice_fusion.refs_0_), channel_id=1, source_target_pairs={{0,64},{32,96},{64,0},{96,32},{1,65},{33,97},{65,1},{97,33},{2,66}... | collective-permute-start | bytes 786440 | tf_op jit(solution)/shard_map/ppermute | solution.py:163
  26.7 14.3 %collective-permute-start.18 = (bf16[264,512]{1,0:T(8,128)(2,1)S(1)}, bf16[264,512]{1,0:T(8,128)(2,1)S(1)}, u32[]{:S(2)}, u32[]{:S(2)}) collective-permute-start(bf16[264,512]{1,0:T(8,128)(2,1)S(1)} %collective-permute-done.5.refs_4_), channel_id=1, source_target_pairs={{0,16},{16,0},{1,17},{17,1},{2,18},{18,2},{3,19},{19,3},{4,20},{20... | collective-permute-start | bytes 811016 | tf_op jit(solution)/shard_map/ppermute | solution.py:20
  29.3 11.6 %collective-permute-start.7 = (bf16[264,512]{1,0:T(8,128)(2,1)S(1)}, bf16[264,512]{1,0:T(8,128)(2,1)S(1)}, u32[]{:S(2)}, u32[]{:S(2)}) collective-permute-start(bf16[264,512]{1,0:T(8,128)(2,1)S(1)} %collective-permute-done.6.refs_4_), channel_id=1, source_target_pairs={{0,2},{2,4},{4,6},{6,8},{8,10},{10,12},{12,14},{14,0},{16,30},{18,... | collective-permute-start | bytes 811016 | tf_op jit(solution)/shard_map/ppermute | solution.py:32
  29.7 9.7 %collective-permute-start.3 = (bf16[256,512]{1,0:T(8,128)(2,1)S(1)}, bf16[256,512]{1,0:T(8,128)(2,1)S(1)}, u32[]{:S(2)}, u32[]{:S(2)}) collective-permute-start(bf16[256,512]{1,0:T(8,128)(2,1)S(1)} %constant_dynamic-update-slice_fusion.refs_0_), channel_id=1, source_target_pairs={{0,32},{32,64},{64,96},{96,0},{1,33},{33,65},{65,97},{97,1},{2,34}... | collective-permute-start | bytes 786440 | tf_op jit(solution)/shard_map/ppermute | solution.py:163
  36.2 7.5 %collective-permute-start.19 = (bf16[264,512]{1,0:T(8,128)(2,1)S(1)}, bf16[264,512]{1,0:T(8,128)(2,1)S(1)}, u32[]{:S(2)}, u32[]{:S(2)}) collective-permute-start(bf16[264,512]{1,0:T(8,128)(2,1)S(1)} %collective-permute-done.11.refs_5_), channel_id=1, source_target_pairs={{0,16},{16,0},{1,17},{17,1},{2,18},{18,2},{3,19},{19,3},{4,20},{20... | collective-permute-start | bytes 811016 | tf_op jit(solution)/shard_map/ppermute | solution.py:20
  37.3 8.1 %collective-permute-start.13 = (bf16[264,512]{1,0:T(8,128)(2,1)S(1)}, bf16[264,512]{1,0:T(8,128)(2,1)S(1)}, u32[]{:S(2)}, u32[]{:S(2)}) collective-permute-start(bf16[264,512]{1,0:T(8,128)(2,1)S(1)} %collective-permute-done.12.refs_5_), channel_id=1, source_target_pairs={{0,2},{2,4},{4,6},{6,8},{8,10},{10,12},{12,14},{14,0},{16,30},{18,... | collective-permute-start | bytes 811016 | tf_op jit(solution)/shard_map/ppermute | solution.py:32
  39.4 9.6 %collective-permute-start.16 = (bf16[264,512]{1,0:T(8,128)(2,1)S(1)}, bf16[264,512]{1,0:T(8,128)(2,1)S(1)}, u32[]{:S(2)}, u32[]{:S(2)}) collective-permute-start(bf16[264,512]{1,0:T(8,128)(2,1)S(1)} %collective-permute-done.6.refs_4_), channel_id=1, source_target_pairs={{0,16},{16,0},{1,17},{17,1},{2,18},{18,2},{3,19},{19,3},{4,20},{20... | collective-permute-start | bytes 811016 | tf_op jit(solution)/shard_map/ppermute | solution.py:20
  41.0 8.0 %collective-permute-start.17 = (bf16[264,512]{1,0:T(8,128)(2,1)S(1)}, bf16[264,512]{1,0:T(8,128)(2,1)S(1)}, u32[]{:S(2)}, u32[]{:S(2)}) collective-permute-start(bf16[264,512]{1,0:T(8,128)(2,1)S(1)} %collective-permute-done.12.refs_5_), channel_id=1, source_target_pairs={{0,16},{16,0},{1,17},{17,1},{2,18},{18,2},{3,19},{19,3},{4,20},{20... | collective-permute-start | bytes 811016 | tf_op jit(solution)/shard_map/ppermute | solution.py:20
  41.0 7.9 %collective-permute-start.8 = (bf16[264,512]{1,0:T(8,128)(2,1)S(1)}, bf16[264,512]{1,0:T(8,128)(2,1)S(1)}, u32[]{:S(2)}, u32[]{:S(2)}) collective-permute-start(bf16[264,512]{1,0:T(8,128)(2,1)S(1)} %collective-permute-done.7.refs_4_), channel_id=1, source_target_pairs={{0,2},{2,4},{4,6},{6,8},{8,10},{10,12},{12,14},{14,0},{16,30},{18,... | collective-permute-start | bytes 811016 | tf_op jit(solution)/shard_map/ppermute | solution.py:32
  43.7 8.3 %collective-permute-start.14 = (bf16[264,512]{1,0:T(8,128)(2,1)S(1)}, bf16[264,512]{1,0:T(8,128)(2,1)S(1)}, u32[]{:S(2)}, u32[]{:S(2)}) collective-permute-start(bf16[264,512]{1,0:T(8,128)(2,1)S(1)} %collective-permute-done.7.refs_4_), channel_id=1, source_target_pairs={{0,16},{16,0},{1,17},{17,1},{2,18},{18,2},{3,19},{19,3},{4,20},{20... | collective-permute-start | bytes 811016 | tf_op jit(solution)/shard_map/ppermute | solution.py:20
  45.4 6.5 %collective-permute-start.15 = (bf16[264,512]{1,0:T(8,128)(2,1)S(1)}, bf16[264,512]{1,0:T(8,128)(2,1)S(1)}, u32[]{:S(2)}, u32[]{:S(2)}) collective-permute-start(bf16[264,512]{1,0:T(8,128)(2,1)S(1)} %collective-permute-done.13.refs_5_), channel_id=1, source_target_pairs={{0,16},{16,0},{1,17},{17,1},{2,18},{18,2},{3,19},{19,3},{4,20},{20... | collective-permute-start | bytes 811016 | tf_op jit(solution)/shard_map/ppermute | solution.py:20
  48.9 7.5 %collective-permute-start.9 = (bf16[264,512]{1,0:T(8,128)(2,1)S(1)}, bf16[264,512]{1,0:T(8,128)(2,1)S(1)}, u32[]{:S(2)}, u32[]{:S(2)}) collective-permute-start(bf16[264,512]{1,0:T(8,128)(2,1)S(1)} %collective-permute-done.8.refs_4_), channel_id=1, source_target_pairs={{0,16},{16,0},{1,17},{17,1},{2,18},{18,2},{3,19},{19,3},{4,20},{20... | collective-permute-start | bytes 811016 | tf_op jit(solution)/shard_map/ppermute | solution.py:20
  91.6 52.8 %copy-start.1 = (bf16[128,512]{1,0:T(8,128)(2,1)}, bf16[128,512]{1,0:T(8,128)(2,1)S(1)}, u32[]{:S(2)}) copy-start(bf16[128,512]{1,0:T(8,128)(2,1)S(1)} %multiply_convert_fusion) | copy-start | bytes 393220
  91.6 1.4 collective-permute-start.20
  93.3 52.9 %copy-start = (bf16[128,512]{1,0:T(8,128)(2,1)S(1)}, bf16[128,512]{1,0:T(8,128)(2,1)}, u32[]{:S(2)}) copy-start(bf16[128,512]{1,0:T(8,128)(2,1)} %param.2) | copy-start | bytes 393220
  144.5 1.6 %collective-permute-start.21 = (bf16[256,512]{1,0:T(8,128)(2,1)S(1)}, bf16[256,512]{1,0:T(8,128)(2,1)S(1)}, u32[]{:S(2)}, u32[]{:S(2)}) collective-permute-start(bf16[256,512]{1,0:T(8,128)(2,1)S(1)} %reshape.38), channel_id=1, source_target_pairs={{0,16},{16,0},{1,17},{17,1},{2,18},{18,2},{3,19},{19,3},{4,20},{20... | collective-permute-start | bytes 786440 | tf_op jit(solution)/shard_map/ppermute | solution.py:20
where the time goes:
time: 150 us; the launch traced here: 147 us
  blocking collectives  84.3 us (56%)
  waiting for transfers between devices  21.4 us (14%)
  starting transfers between devices  21 us (14%)
  Pallas kernels  13.3 us (9%)
  other arithmetic  3.96 us (3%)
  local copies, waits for them, and re-layouts  1.96 us (1%)
    all_to_all x1, blocking collectives, step(): lax.all_to_all(partial, row_axes, 0, 0, tiled=True)  33.5 us
    all_to_all x1, blocking collectives, step(): lax.all_to_all(gram.reshape(chips, -1, 128), chip_axes, 0, 0, tiled=True)  30.1 us
    all_to_all x1, blocking collectives, from_everyone(): return lax.all_to_all(copies, axes, split_axis=0, concat_axis=0, tiled=True)  20.7 us
    pallas_call x6, Pallas kernels, add_tiles(): pl.pallas_call(body, out_shape=out_shape, in_specs=[spec] * len(operands)...  13.3 us
    ppermute x12, starting transfers between devices, swapped(): return lax.ppermute(value, axis, [(0, 1), (1, 0)])  11.6 us
    ppermute x3, waiting for transfers between devices, step(): rows.append(lax.ppermute(rows[0], 'x', pairs))  7.46 us
    ppermute x7, waiting for transfers between devices, along_z(): return lax.ppermute(value, ('c', 'z'), pairs)  7.34 us
    ppermute x12, waiting for transfers between devices, swapped(): return lax.ppermute(value, axis, [(0, 1), (1, 0)])  6.6 us
  transfers between devices with their start and end apart: 22, of which 10 were waited for; matrix products, arithmetic and copies ran while one was open for 1% of the time, Pallas kernels for 8%

commit v1 on v0

--- a/solution.py
+++ b/solution.py
@@ -32,37 +32,100 @@
     return lax.ppermute(value, ("c", "z"), pairs)
 
 
-def extra_rows(features, coefs):
+def beside_y(value):
+    pairs = []
+    for yh in range(2):
+        for c in range(2):
+            for yl in range(2):
+                pairs.append(((yh * 2 + c) * 2 + yl, ((yh ^ c) * 2 + c) * 2 + 1 - yl))
+    return lax.ppermute(value, ("yh", "c", "yl"), pairs)
+
+
+def in_vmem(body, out_shape, *operands, **params):
+    spec = pl.BlockSpec(memory_space=pltpu.VMEM)
+    several = isinstance(out_shape, list)
+    return pl.pallas_call(
+        body,
+        out_shape=out_shape,
+        in_specs=[spec] * len(operands),
+        out_specs=[spec] * len(out_shape) if several else spec,
+        compiler_params=pltpu.CompilerParams(vmem_limit_bytes=VMEM_LIMIT),
+        **params,
+    )(*operands)
+
+
+def pack_kernel(features_ref, coefs_ref, out_ref):
+    points, width = features_ref.shape
+    features = features_ref[...]
     full = features.astype(F32)
-    norms = jnp.sum(full * full, axis=1)
-    high = lax.reduce_precision(norms, 8, 7)
-    middle = lax.reduce_precision(norms - high, 8, 7)
-    low = lax.reduce_precision(norms - high - middle, 8, 7)
-    rows = jnp.stack([coefs.astype(F32), high, middle, low]).astype(BF16)
-    return jnp.pad(rows, ((0, EXTRA - 4), (0, 0)))
-
-
-def widened(rows, width):
-    return jnp.pad(rows, ((0, 0), (0, width - rows.shape[1])))
+    square = full * full
+    high = square.astype(BF16)
+    low = (square - high.astype(F32)).astype(BF16)
+    ones = jnp.ones((EXTRA, width), BF16)
+    norms = sum(
+        lax.dot_general(ones, part, (((1,), (1,)), ((), ())), preferred_element_type=F32)
+        for part in (high, low)
+    )
+    pieces, rest = [coefs_ref[...].astype(F32)], norms
+    for _ in range(3):
+        pieces.append(rest.astype(BF16).astype(F32))
+        rest = rest - pieces[-1]
+    row = lax.broadcasted_iota(jnp.int32, (EXTRA, points), 0)
+    extra = jnp.zeros((EXTRA, points), F32)
+    for at, piece in enumerate(pieces):
+        extra = jnp.where(row == at, piece, extra)
+    out_ref[:points, :] = features
+    out_ref[points:, :] = jnp.zeros((EXTRA, width), BF16)
+    out_ref[points:, :points] = extra.astype(BF16)
+
+
+def pair_kernel(near_ref, other_ref, out_ref):
+    width = near_ref.shape[1]
+    points = near_ref.shape[0] - EXTRA
+    out_ref[2 * points :, :] = jnp.zeros((EXTRA, width), BF16)
+    for at, ref in enumerate((near_ref, other_ref)):
+        here = slice(at * points, (at + 1) * points)
+        out_ref[here, :] = ref[:points, :]
+        out_ref[2 * points :, here] = ref[points:, :points]
 
 
 def pair_block(features, coefs):
     points, width = features.shape
-    extras = extra_rows(features, coefs)
-    block = jnp.concatenate([features, widened(extras, width)])
+    shape = jax.ShapeDtypeStruct((points + EXTRA, width), BF16)
+    block = in_vmem(pack_kernel, shape, features, coefs.reshape(1, -1))
     other = swapped(block, "yh")
-    extras = jnp.concatenate([extras, other[points:, :points]], axis=1)
-    return jnp.concatenate([features, other[:points], widened(extras, width)])
-
-
-def tile_kernel(first, last, row_refs_count, chunk_count, *refs):
+    shape = jax.ShapeDtypeStruct((2 * points + EXTRA, width), BF16)
+    return in_vmem(pair_kernel, shape, block, other)
+
+
+def recolor_kernel(features_ref, own_ref, other_ref, out_ref):
+    half = own_ref.shape[0]
+    core = lax.axis_index("c")
+
+    def store(upper_ref, lower_ref):
+        out = jnp.dot(features_ref[:, :half], upper_ref[...], preferred_element_type=F32)
+        out = out + jnp.dot(features_ref[:, half:], lower_ref[...], preferred_element_type=F32)
+        out_ref[...] = out.astype(BF16)
+
+    @pl.when(core == 0)
+    def _():
+        store(own_ref, other_ref)
+
+    @pl.when(core != 0)
+    def _():
+        store(other_ref, own_ref)
+
+
+def tile_kernel(first, sides, row_refs_count, chunk_count, *refs):
+    last = len(sides) == 1
     row_refs, refs = refs[:row_refs_count], refs[row_refs_count:]
     chunk_refs, refs = refs[:chunk_count], refs[chunk_count:]
     if not first:
         old_ref, old_totals_ref, *refs = refs
-    out_ref, refs = refs[0], refs[1:]
-    if not last:
-        totals_ref, refs = refs[0], refs[1:]
+    if last:
+        out_refs, refs = refs[:row_refs_count], refs[row_refs_count:]
+    else:
+        out_ref, totals_ref, *refs = refs
     (weighted_ref,) = refs
     row_count, width = row_refs[0].shape
     points = chunk_refs[0].shape[0] - EXTRA
@@ -77,10 +140,11 @@
                 spread, ref[k : k + LANES, :], preferred_element_type=F32
             ).astype(BF16)
 
-    for s in range(0, row_refs_count, 2):
-        strip = 2 * row_count
-        here = slice(s * row_count, s * row_count + strip)
-        rows = jnp.concatenate([row_refs[s][...], row_refs[s + 1][...]])
+    shard = row_count // 2
+    strip = row_refs_count * shard
+    for side in sides:
+        here = slice(side * strip, (side + 1) * strip)
+        rows = jnp.concatenate([ref[side * shard : (side + 1) * shard] for ref in row_refs])
         full = rows.astype(F32)
         row_terms = jnp.sum(full * full, axis=1, keepdims=True) * (-scale)
         totals = jnp.zeros((strip, LANES), F32) if first else old_totals_ref[here, :]
@@ -103,25 +167,22 @@
             moments = moments + old_ref[here, :]
         if last:
             moments = moments - jnp.sum(totals, axis=1, keepdims=True) * full
-            x_at, yl_at = lax.axis_index("x"), lax.axis_index("yl")
-            for k in range(0, strip, LANES):
-                away, beside = divmod((here.start + k) // LANES, 2)
-                place = 2 * lax.rem(x_at + away, row_refs_count) + lax.rem(yl_at + beside, 2)
-                out_ref[place] = moments[k : k + LANES]
+            for at, ref in enumerate(out_refs):
+                ref[...] = moments[at * shard : (at + 1) * shard]
         else:
             out_ref[here, :] = moments
             totals_ref[here, :] = totals
 
 
-def add_tiles(rows, chunks, carried, last):
-    row_count, width = sum(r.shape[0] for r in rows), rows[0].shape[1]
+def add_tiles(rows, chunks, carried, sides=(0, 1)):
+    width = rows[0].shape[1]
+    row_count = sum(r.shape[0] for r in rows) * len(sides) // 2
     columns = sum(chunk.shape[0] - EXTRA for chunk in chunks)
-    first = carried is None
-    spec = pl.BlockSpec(memory_space=pltpu.VMEM)
+    first, last = carried is None, len(sides) == 1
     operands = [*rows, *chunks] + ([] if first else list(carried))
     aliases = {}
     if last:
-        out_shape = [jax.ShapeDtypeStruct((row_count // LANES, LANES, width), F32)]
+        out_shape = [jax.ShapeDtypeStruct((row_count // len(rows), width), F32)] * len(rows)
     else:
         out_shape = [
             jax.ShapeDtypeStruct((row_count, width), F32),
@@ -131,31 +192,44 @@
             aliases = {len(operands) - 2: 0, len(operands) - 1: 1}
 
     def body(*refs):
-        tile_kernel(first, last, len(rows), len(chunks), *refs)
-
-    return pl.pallas_call(
+        tile_kernel(first, sides, len(rows), len(chunks), *refs)
+
+    return in_vmem(
         body,
-        out_shape=out_shape,
-        in_specs=[spec] * len(operands),
-        out_specs=[spec] * len(out_shape),
+        out_shape,
+        *operands,
         scratch_shapes=[pltpu.VMEM((columns, width), BF16)],
         input_output_aliases=aliases,
-        compiler_params=pltpu.CompilerParams(vmem_limit_bytes=VMEM_LIMIT),
         cost_estimate=pl.CostEstimate(
             flops=4 * row_count * columns * width,
             bytes_accessed=4 * row_count * width,
             transcendentals=row_count * columns,
         ),
-    )(*operands)
+    )
+
+
+def summed_partials(own, beside):
+    count = len(own)
+    totals = [None] * count
+    parts = []
+    for at in ((2, 1), (3, 0)):
+        parts.append((at, beside_y(jnp.stack([beside[k] for k in at]))))
+    for at, part in parts:
+        for i, k in enumerate(at):
+            totals[k] = own[k] + part[i]
+    result = totals[0]
+    for k in (2, 1, 3):
+        pairs = [(x, (x + k) % count) for x in range(count)]
+        result = result + lax.ppermute(totals[k], "x", pairs)
+    return result
 
 
 def step(features, coefs):
     points, width = features.shape
     gamma = 2.0 / width
-    row_axes = ("x", "yl")
     chip_axes = ("yh", "x", "z", "yl")
 
-    beside = swapped(features, "yl")
+    beside = beside_y(features)
     rows = [jnp.concatenate([features, beside])]
     x_count = lax.axis_size("x")
     for shift in range(1, x_count):
@@ -176,11 +250,11 @@
         groups.append([near, far, other_near, other_far])
 
     carried = None
-    for at, group in enumerate(groups):
-        carried = add_tiles(rows, group, carried, at == len(groups) - 1)
-    (partial,) = carried
-    summed = jnp.sum(lax.all_to_all(partial, row_axes, 0, 0, tiled=True), axis=0)
-    grads = (2.0 * gamma * summed).astype(BF16)
+    for group in groups[:-1]:
+        carried = add_tiles(rows, group, carried)
+    beside = add_tiles(rows, groups[-1], carried, sides=(1,))
+    own = add_tiles(rows, groups[-1], carried, sides=(0,))
+    grads = (2.0 * gamma * summed_partials(own, beside)).astype(BF16)
 
     core = lax.axis_index("c")
     half = width // 2
@@ -193,11 +267,10 @@
     own_agop = (jnp.sum(parts, axis=0) / point_count).astype(BF16)
     own_rows = from_everyone(own_agop, chip_axes).reshape(half, width)
     other_rows = swapped(own_rows, "c")
-    upper = jnp.where(core == 0, own_rows, other_rows)
-    lower = jnp.where(core == 0, other_rows, own_rows)
-    agop = jnp.concatenate([upper, lower])
-    recolored = jnp.dot(features, agop, preferred_element_type=F32)
-    return grads, recolored.astype(BF16)
+    recolored = in_vmem(
+        recolor_kernel, jax.ShapeDtypeStruct((points, width), BF16), features, own_rows, other_rows
+    )
+    return grads, recolored
 
 
 def solution(mesh):

time: 150 us -> 142 us (0.947)
  blocking collectives: 84.3 us -> 51.4 us
  starting transfers between devices: 21 us -> 36.2 us
  waiting for transfers between devices: 21.4 us -> 32.9 us
  other arithmetic: 3.96 us -> 0.46 us
  Pallas kernels: 13.3 us -> 14.8 us
    all_to_all x1 -> x0, blocking collectives: 33.5 us -> none  [step(): lax.all_to_all(partial, row_axes, 0, 0, tiled=True)]
    ppermute x0 -> x6, waiting for transfers between devices: none -> 13.9 us  [the longest x3 7.55 us: summed_partials(): result = result + lax.ppermute(totals[k], 'x', pairs)]
    ppermute x0 -> x6, starting transfers between devices: none -> 13.1 us  [the longest x3 9.3 us: summed_partials(): result = result + lax.ppermute(totals[k], 'x', pairs)]
    ppermute x7, starting transfers between devices: 5.15 us -> 9.12 us  [along_z(): return lax.ppermute(value, ('c', 'z'), pairs)]
    concatenate x3 -> x0, other arithmetic: 1.85 us -> none  [the longest x1 0.93 us: pair_block(): return jnp.concatenate([features, other[:points], widened(extras, width)])]
    ppermute x12 -> x11, starting transfers between devices: 11.6 us -> 9.82 us  [swapped(): return lax.ppermute(value, axis, [(0, 1), (1, 0)])]
    pallas_call x6 -> x10, Pallas kernels: 13.3 us -> 14.8 us  [in_vmem(): pl.pallas_call(body, out_shape=out_shape, in_specs=[spec] * len(operands)...]
    ppermute x12 -> x11, waiting for transfers between devices: 6.6 us -> 6.5 us  [swapped(): return lax.ppermute(value, axis, [(0, 1), (1, 0)])]
  transfers between devices with their start and end apart: 22 -> 27, of which waited for: 10 -> 14; matrix products, arithmetic and copies ran while one was open for 1% -> 1% of each run, Pallas kernels for 8% -> 9%
where the time goes in v1:
time: 142 us; the launch traced here: 140 us
  blocking collectives  51.4 us (36%)
  starting transfers between devices  36.2 us (25%)
  waiting for transfers between devices  32.9 us (23%)
  Pallas kernels  14.8 us (10%)
  local copies, waits for them, and re-layouts  2.73 us (2%)
    all_to_all x1, blocking collectives, step(): lax.all_to_all(gram.reshape(chips, -1, 128), chip_axes, 0, 0, tiled=True)  30.7 us
    all_to_all x1, blocking collectives, from_everyone(): return lax.all_to_all(copies, axes, split_axis=0, concat_axis=0, tiled=True)  20.7 us
    pallas_call x10, Pallas kernels, in_vmem(): pl.pallas_call(body, out_shape=out_shape, in_specs=[spec] * len(operands)...  14.8 us
    ppermute x11, starting transfers between devices, swapped(): return lax.ppermute(value, axis, [(0, 1), (1, 0)])  9.82 us
    ppermute x3, starting transfers between devices, summed_partials(): result = result + lax.ppermute(totals[k], 'x', pairs)  9.3 us
    ppermute x7, starting transfers between devices, along_z(): return lax.ppermute(value, ('c', 'z'), pairs)  9.12 us
    ppermute x3, waiting for transfers between devices, summed_partials(): result = result + lax.ppermute(totals[k], 'x', pairs)  7.55 us
    ppermute x11, waiting for transfers between devices, swapped(): return lax.ppermute(value, axis, [(0, 1), (1, 0)])  6.5 us
  transfers between devices with their start and end apart: 27, of which 14 were waited for; matrix products, arithmetic and copies ran while one was open for 1% of the time, Pallas kernels for 9%

profile of v1, /device:TPU:2, one launch (start us, length us, event | category | flops | bytes accessed | tf_op | source)
XLA Modules:
  0.0 139.6 jit_solution(14352466208062065921)
XLA Ops:
  0.6 0.0 copy-start
  0.6 0.9 copy-done
  1.5 0.7 copy-done.2
  2.2 0.2 shard_map.41.near_ref
  2.4 3.2 %collective-permute-start.4 = (bf16[136,512]{1,0:T(8,128)(2,1)S(1)}, bf16[136,512]{1,0:T(8,128)(2,1)S(1)}, u32[]{:S(2)}, u32[]{:S(2)}) collective-permute-start(bf16[136,512]{1,0:T(8,128)(2,1)S(1)} %shard_map.41.near_ref), channel_id=1, source_target_pairs={{0,128},{128,0},{1,129},{129,1},{2,130},{130,2},{3,131},{131,3},{4... | collective-permute-start | bytes 417800 | tf_op jit(solution)/shard_map/ppermute | solution.py:20
  5.6 3.7 %collective-permute-done.4.other_ref = bf16[136,512]{1,0:T(8,128)(2,1)S(1)} collective-permute-done((bf16[136,512]{1,0:T(8,128)(2,1)S(1)}, bf16[136,512]{1,0:T(8,128)(2,1)S(1)}, u32[]{:S(2)}, u32[]{:S(2)}) %collective-permute-start.4) | collective-permute-done | bytes 139296 | tf_op jit(solution)/shard_map/ppermute | solution.py:20
  9.4 0.1 collective-permute-start.10
  9.5 2.0 %collective-permute-start.5 = (bf16[264,512]{1,0:T(8,128)(2,1)S(1)}, bf16[264,512]{1,0:T(8,128)(2,1)S(1)}, u32[]{:S(2)}, u32[]{:S(2)}) collective-permute-start(bf16[264,512]{1,0:T(8,128)(2,1)S(1)} %shard_map.42.refs_4_), channel_id=1, source_target_pairs={{0,2},{2,4},{4,6},{6,8},{8,10},{10,12},{12,14},{14,0},{16,30},{18,... | collective-permute-start | bytes 811016 | tf_op jit(solution)/shard_map/ppermute | solution.py:32
  11.4 1.6 %collective-permute-start = (bf16[128,512]{1,0:T(8,128)(2,1)}, bf16[128,512]{1,0:T(8,128)(2,1)S(1)}, u32[]{:S(2)}, u32[]{:S(2)}) collective-permute-start(bf16[128,512]{1,0:T(8,128)(2,1)} %features_ref.3), channel_id=1, source_target_pairs={{0,1},{1,0},{16,145},{17,144},{128,129},{129,128},{144,17},{145,16... | collective-permute-start | bytes 393224 | tf_op jit(solution)/shard_map/ppermute | solution.py:41
  13.0 1.9 %collective-permute-start.11 = (bf16[264,512]{1,0:T(8,128)(2,1)S(1)}, bf16[264,512]{1,0:T(8,128)(2,1)S(1)}, u32[]{:S(2)}, u32[]{:S(2)}) collective-permute-start(bf16[264,512]{1,0:T(8,128)(2,1)S(1)} %collective-permute-done.10.refs_5_), channel_id=1, source_target_pairs={{0,2},{2,4},{4,6},{6,8},{8,10},{10,12},{12,14},{14,0},{16,30},{18,... | collective-permute-start | bytes 811016 | tf_op jit(solution)/shard_map/ppermute | solution.py:32
  14.9 0.9 constant_dynamic-update-slice_fusion.1
  15.9 4.0 %collective-permute-done.5.refs_4_ = bf16[264,512]{1,0:T(8,128)(2,1)S(1)} collective-permute-done((bf16[264,512]{1,0:T(8,128)(2,1)S(1)}, bf16[264,512]{1,0:T(8,128)(2,1)S(1)}, u32[]{:S(2)}, u32[]{:S(2)}) %collective-permute-start.5) | collective-permute-done | bytes 270368 | tf_op jit(solution)/shard_map/ppermute | solution.py:32
  19.8 0.0 collective-permute-start.6
  19.8 0.0 collective-permute-done
  19.8 0.6 collective-permute-start.1
  20.5 2.3 %collective-permute-done.11.refs_5_ = bf16[264,512]{1,0:T(8,128)(2,1)S(1)} collective-permute-done((bf16[264,512]{1,0:T(8,128)(2,1)S(1)}, bf16[264,512]{1,0:T(8,128)(2,1)S(1)}, u32[]{:S(2)}, u32[]{:S(2)}) %collective-permute-start.11) | collective-permute-done | bytes 270368 | tf_op jit(solution)/shard_map/ppermute | solution.py:32
  22.7 0.0 collective-permute-start.12
  22.7 2.1 %collective-permute-start.2 = (bf16[256,512]{1,0:T(8,128)(2,1)S(1)}, bf16[256,512]{1,0:T(8,128)(2,1)S(1)}, u32[]{:S(2)}, u32[]{:S(2)}) collective-permute-start(bf16[256,512]{1,0:T(8,128)(2,1)S(1)} %constant_dynamic-update-slice_fusion.refs_0_), channel_id=1, source_target_pairs={{0,64},{32,96},{64,0},{96,32},{1,65},{33,97},{65,1},{97,33},{2,66}... | collective-permute-start | bytes 786440 | tf_op jit(solution)/shard_map/ppermute | solution.py:237
  24.8 2.5 %collective-permute-start.18 = (bf16[264,512]{1,0:T(8,128)(2,1)S(1)}, bf16[264,512]{1,0:T(8,128)(2,1)S(1)}, u32[]{:S(2)}, u32[]{:S(2)}) collective-permute-start(bf16[264,512]{1,0:T(8,128)(2,1)S(1)} %collective-permute-done.5.refs_4_), channel_id=1, source_target_pairs={{0,16},{16,0},{1,17},{17,1},{2,18},{18,2},{3,19},{19,3},{4,20},{20... | collective-permute-start | bytes 811016 | tf_op jit(solution)/shard_map/ppermute | solution.py:20
  27.4 0.1 collective-permute-done.6.refs_4_
  27.5 0.0 collective-permute-start.7
  27.5 0.4 collective-permute-done.1.refs_1_
  27.9 1.5 %collective-permute-start.3 = (bf16[256,512]{1,0:T(8,128)(2,1)S(1)}, bf16[256,512]{1,0:T(8,128)(2,1)S(1)}, u32[]{:S(2)}, u32[]{:S(2)}) collective-permute-start(bf16[256,512]{1,0:T(8,128)(2,1)S(1)} %constant_dynamic-update-slice_fusion.refs_0_), channel_id=1, source_target_pairs={{0,32},{32,64},{64,96},{96,0},{1,33},{33,65},{65,97},{97,1},{2,34}... | collective-permute-start | bytes 786440 | tf_op jit(solution)/shard_map/ppermute | solution.py:237
  29.3 5.1 %collective-permute-done.2.refs_2_ = bf16[256,512]{1,0:T(8,128)(2,1)S(1)} collective-permute-done((bf16[256,512]{1,0:T(8,128)(2,1)S(1)}, bf16[256,512]{1,0:T(8,128)(2,1)S(1)}, u32[]{:S(2)}, u32[]{:S(2)}) %collective-permute-start.2) | collective-permute-done | bytes 262176 | tf_op jit(solution)/shard_map/ppermute | solution.py:237
  34.4 1.1 collective-permute-start.19
  35.5 1.1 collective-permute-start.13
  36.6 0.7 collective-permute-done.3.refs_3_
  37.3 1.8 %collective-permute-start.16 = (bf16[264,512]{1,0:T(8,128)(2,1)S(1)}, bf16[264,512]{1,0:T(8,128)(2,1)S(1)}, u32[]{:S(2)}, u32[]{:S(2)}) collective-permute-start(bf16[264,512]{1,0:T(8,128)(2,1)S(1)} %collective-permute-done.6.refs_4_), channel_id=1, source_target_pairs={{0,16},{16,0},{1,17},{17,1},{2,18},{18,2},{3,19},{19,3},{4,20},{20... | collective-permute-start | bytes 811016 | tf_op jit(solution)/shard_map/ppermute | solution.py:20
  39.1 0.0 collective-permute-start.17
  39.1 4.1 %collective-permute-start.8 = (bf16[264,512]{1,0:T(8,128)(2,1)S(1)}, bf16[264,512]{1,0:T(8,128)(2,1)S(1)}, u32[]{:S(2)}, u32[]{:S(2)}) collective-permute-start(bf16[264,512]{1,0:T(8,128)(2,1)S(1)} %collective-permute-done.7.refs_4_), channel_id=1, source_target_pairs={{0,2},{2,4},{4,6},{6,8},{8,10},{10,12},{12,14},{14,0},{16,30},{18,... | collective-permute-start | bytes 811016 | tf_op jit(solution)/shard_map/ppermute | solution.py:32
  43.2 1.6 %shard_map.43 = (f32[1024,512]{1,0:T(8,128)S(1)}, f32[1024,128]{1,0:T(8,128)S(1)}) custom-call(bf16[256,512]{1,0:T(8,128)(2,1)S(1)} %constant_dynamic-update-slice_fusion.refs_0_, bf16[256,512]{1,0:T(8,128)(2,1)S(1)} %collective-permute-done.1.refs_1_, bf16[256,512]{1,0:T(8,128)(2,1)S(1)} %collective-permute-done.2.refs_2_, ...), custom_call_target="tpu_custom_call" | custom-call | flops 1073741824 | bytes 2097152 | tf_op jit(solution)/shard_map/pallas_call | solution.py:47
  44.8 0.1 collective-permute-start.14
  44.9 0.5 collective-permute-start.15
  45.4 3.0 %shard_map.44 = (f32[1024,512]{1,0:T(8,128)S(1)}, f32[1024,128]{1,0:T(8,128)S(1)}) custom-call(bf16[256,512]{1,0:T(8,128)(2,1)S(1)} %constant_dynamic-update-slice_fusion.refs_0_, bf16[256,512]{1,0:T(8,128)(2,1)S(1)} %collective-permute-done.1.refs_1_, ...), custom_call_target="tpu_custom_call", output_to_operand_aliasing={{0}: (8, {}), {1}: (9, {})} | custom-call | flops 2147483648 | bytes 2097152 | tf_op jit(solution)/shard_map/pallas_call | solution.py:47
  48.4 0.2 collective-permute-start.9
  48.6 3.0 %shard_map.45 = (f32[1024,512]{1,0:T(8,128)S(1)}, f32[1024,128]{1,0:T(8,128)S(1)}) custom-call(bf16[256,512]{1,0:T(8,128)(2,1)S(1)} %constant_dynamic-update-slice_fusion.refs_0_, bf16[256,512]{1,0:T(8,128)(2,1)S(1)} %collective-permute-done.1.refs_1_, ...), custom_call_target="tpu_custom_call", output_to_operand_aliasing={{0}: (8, {}), {1}: (9, {})} | custom-call | flops 2147483648 | bytes 2097152 | tf_op jit(solution)/shard_map/pallas_call | solution.py:47
  51.7 3.0 %shard_map.46 = (f32[1024,512]{1,0:T(8,128)S(1)}, f32[1024,128]{1,0:T(8,128)S(1)}) custom-call(bf16[256,512]{1,0:T(8,128)(2,1)S(1)} %constant_dynamic-update-slice_fusion.refs_0_, bf16[256,512]{1,0:T(8,128)(2,1)S(1)} %collective-permute-done.1.refs_1_, ...), custom_call_target="tpu_custom_call", output_to_operand_aliasing={{0}: (8, {}), {1}: (9, {})} | custom-call | flops 2147483648 | bytes 2097152 | tf_op jit(solution)/shard_map/pallas_call | solution.py:47
  54.7 1.5 %shard_map.47 = (f32[1024,512]{1,0:T(8,128)S(1)}, f32[1024,128]{1,0:T(8,128)S(1)}) custom-call(bf16[256,512]{1,0:T(8,128)(2,1)S(1)} %constant_dynamic-update-slice_fusion.refs_0_, bf16[256,512]{1,0:T(8,128)(2,1)S(1)} %collective-permute-done.1.refs_1_, ...), custom_call_target="tpu_custom_call", output_to_operand_aliasing={{0}: (5, {}), {1}: (6, {})} | custom-call | flops 536870912 | bytes 2097152 | tf_op jit(solution)/shard_map/pallas_call | solution.py:47
  56.2 0.8 shard_map.49
  57.1 0.7 collective-permute-start.21
  57.8 1.5 %collective-permute-start.20 = (f32[2,128,512]{2,1,0:T(8,128)S(1)}, f32[2,128,512]{2,1,0:T(8,128)S(1)}, u32[]{:S(2)}, u32[]{:S(2)}) collective-permute-start(f32[2,128,512]{2,1,0:T(8,128)S(1)} %pad_maximum_fusion), channel_id=1, source_target_pairs={{0,1},{1,0},{16,145},{17,144},{128,129},{129,128},{144,17},{145,16... | collective-permute-start | bytes 1572872 | tf_op jit(solution)/shard_map/ppermute | solution.py:41
  59.3 0.8 shard_map.48
  60.1 6.2 %collective-permute-done.21 = f32[2,128,512]{2,1,0:T(8,128)S(1)} collective-permute-done((f32[2,128,512]{2,1,0:T(8,128)S(1)}, f32[2,128,512]{2,1,0:T(8,128)S(1)}, u32[]{:S(2)}, u32[]{:S(2)}) %collective-permute-start.21) | collective-permute-done | bytes 524320 | tf_op jit(solution)/shard_map/ppermute | solution.py:41
  66.3 0.1 fusion.3
  66.4 4.5 %collective-permute-start.22 = (f32[128,512]{1,0:T(8,128)S(1)}, f32[128,512]{1,0:T(8,128)S(1)}, u32[]{:S(2)}, u32[]{:S(2)}) collective-permute-start(f32[128,512]{1,0:T(8,128)S(1)} %get-tuple-element.38), channel_id=1, source_target_pairs={{0,64},{32,96},{64,0},{96,32},{1,65},{33,97},{65,1},{97,33},{2,66}... | collective-permute-start | bytes 786440 | tf_op jit(solution)/shard_map/ppermute | solution.py:223
  70.9 0.9 collective-permute-start.23
  71.8 0.1 collective-permute-done.20
  72.0 3.9 %collective-permute-start.24 = (f32[128,512]{1,0:T(8,128)S(1)}, f32[128,512]{1,0:T(8,128)S(1)}, u32[]{:S(2)}, u32[]{:S(2)}) collective-permute-start(f32[128,512]{1,0:T(8,128)S(1)} %fusion.1), channel_id=1, source_target_pairs={{0,96},{32,0},{64,32},{96,64},{1,97},{33,1},{65,33},{97,65},{2,98}... | collective-permute-start | bytes 786440 | tf_op jit(solution)/shard_map/ppermute | solution.py:223
  75.9 2.0 %collective-permute-done.22 = f32[128,512]{1,0:T(8,128)S(1)} collective-permute-done((f32[128,512]{1,0:T(8,128)S(1)}, f32[128,512]{1,0:T(8,128)S(1)}, u32[]{:S(2)}, u32[]{:S(2)}) %collective-permute-start.22) | collective-permute-done | bytes 262176 | tf_op jit(solution)/shard_map/ppermute | solution.py:223
  78.0 5.4 %collective-permute-done.23 = f32[128,512]{1,0:T(8,128)S(1)} collective-permute-done((f32[128,512]{1,0:T(8,128)S(1)}, f32[128,512]{1,0:T(8,128)S(1)}, u32[]{:S(2)}, u32[]{:S(2)}) %collective-permute-start.23) | collective-permute-done | bytes 262176 | tf_op jit(solution)/shard_map/ppermute | solution.py:223
  83.4 0.1 collective-permute-done.24
  83.5 0.1 fusion.9
  83.6 0.0 copy-start.3
  83.6 0.2 collective-permute-start.25
  83.8 1.2 collective-permute-done.25
  85.1 0.2 fusion
  85.3 0.0 copy-start.1
  85.4 30.7 %all_to_all.10 = f32[128,8,128]{2,1,0:T(8,128)S(1)} all-to-all(f32[128,8,128]{2,1,0:T(8,128)S(1)} %reshape.14), channel_id=1, replica_groups=mesh['yh'=2,'x'=4,'c'=2,'z'=8,'yl'=2] {'yh','x','z','yl'}, dimensions={0} | all-to-all | bytes 1048576 | tf_op jit(solution)/shard_map/all_to_all | solution.py:265
  116.0 0.1 reduce_sum.9
  116.2 20.7 %all_to_all.11 = bf16[128,8,128]{2,1,0:T(8,128)(2,1)S(1)} all-to-all(bf16[128,8,128]{2,1,0:T(8,128)(2,1)S(1)} %broadcast_in_dim.3), channel_id=1, replica_groups=mesh['yh'=2,'x'=4,'c'=2,'z'=8,'yl'=2] {'yh','x','z','yl'}, dimensions={0} | all-to-all | bytes 524288 | tf_op jit(solution)/shard_map/all_to_all | solution.py:25
  136.9 0.2 reshape.15.own_ref
  137.1 0.1 collective-permute-start.26
  137.2 1.5 %collective-permute-done.26.other_ref = bf16[256,512]{1,0:T(8,128)(2,1)S(1)} collective-permute-done((bf16[256,512]{1,0:T(8,128)(2,1)S(1)}, bf16[256,512]{1,0:T(8,128)(2,1)S(1)}, u32[]{:S(2)}, u32[]{:S(2)}) %collective-permute-start.26) | collective-permute-done | bytes 262176 | tf_op jit(solution)/shard_map/ppermute | solution.py:20
  138.7 0.9 shard_map.50
  (23 shorter events, 0.3 us)
Async XLA Ops:
  0.6 0.9 copy-start
  1.5 0.7 copy-start.2
  2.4 7.0 %collective-permute-start.4 = (bf16[136,512]{1,0:T(8,128)(2,1)S(1)}, bf16[136,512]{1,0:T(8,128)(2,1)S(1)}, u32[]{:S(2)}, u32[]{:S(2)}) collective-permute-start(bf16[136,512]{1,0:T(8,128)(2,1)S(1)} %shard_map.41.near_ref), channel_id=1, source_target_pairs={{0,128},{128,0},{1,129},{129,1},{2,130},{130,2},{3,131},{131,3},{4... | collective-permute-start | bytes 417800 | tf_op jit(solution)/shard_map/ppermute | solution.py:20
  9.4 3.7 %collective-permute-start.10 = (bf16[264,512]{1,0:T(8,128)(2,1)S(1)}, bf16[264,512]{1,0:T(8,128)(2,1)S(1)}, u32[]{:S(2)}, u32[]{:S(2)}) collective-permute-start(bf16[264,512]{1,0:T(8,128)(2,1)S(1)} %shard_map.42.refs_4_), channel_id=1, source_target_pairs={{0,16},{16,0},{1,17},{17,1},{2,18},{18,2},{3,19},{19,3},{4,20},{20... | collective-permute-start | bytes 811016 | tf_op jit(solution)/shard_map/ppermute | solution.py:20
  9.5 10.4 %collective-permute-start.5 = (bf16[264,512]{1,0:T(8,128)(2,1)S(1)}, bf16[264,512]{1,0:T(8,128)(2,1)S(1)}, u32[]{:S(2)}, u32[]{:S(2)}) collective-permute-start(bf16[264,512]{1,0:T(8,128)(2,1)S(1)} %shard_map.42.refs_4_), channel_id=1, source_target_pairs={{0,2},{2,4},{4,6},{6,8},{8,10},{10,12},{12,14},{14,0},{16,30},{18,... | collective-permute-start | bytes 811016 | tf_op jit(solution)/shard_map/ppermute | solution.py:32
  11.4 8.4 %collective-permute-start = (bf16[128,512]{1,0:T(8,128)(2,1)}, bf16[128,512]{1,0:T(8,128)(2,1)S(1)}, u32[]{:S(2)}, u32[]{:S(2)}) collective-permute-start(bf16[128,512]{1,0:T(8,128)(2,1)} %features_ref.3), channel_id=1, source_target_pairs={{0,1},{1,0},{16,145},{17,144},{128,129},{129,128},{144,17},{145,16... | collective-permute-start | bytes 393224 | tf_op jit(solution)/shard_map/ppermute | solution.py:41
  13.0 9.7 %collective-permute-start.11 = (bf16[264,512]{1,0:T(8,128)(2,1)S(1)}, bf16[264,512]{1,0:T(8,128)(2,1)S(1)}, u32[]{:S(2)}, u32[]{:S(2)}) collective-permute-start(bf16[264,512]{1,0:T(8,128)(2,1)S(1)} %collective-permute-done.10.refs_5_), channel_id=1, source_target_pairs={{0,2},{2,4},{4,6},{6,8},{8,10},{10,12},{12,14},{14,0},{16,30},{18,... | collective-permute-start | bytes 811016 | tf_op jit(solution)/shard_map/ppermute | solution.py:32
  19.8 7.7 %collective-permute-start.6 = (bf16[264,512]{1,0:T(8,128)(2,1)S(1)}, bf16[264,512]{1,0:T(8,128)(2,1)S(1)}, u32[]{:S(2)}, u32[]{:S(2)}) collective-permute-start(bf16[264,512]{1,0:T(8,128)(2,1)S(1)} %collective-permute-done.5.refs_4_), channel_id=1, source_target_pairs={{0,2},{2,4},{4,6},{6,8},{8,10},{10,12},{12,14},{14,0},{16,30},{18,... | collective-permute-start | bytes 811016 | tf_op jit(solution)/shard_map/ppermute | solution.py:32
  19.8 8.0 %collective-permute-start.1 = (bf16[256,512]{1,0:T(8,128)(2,1)S(1)}, bf16[256,512]{1,0:T(8,128)(2,1)S(1)}, u32[]{:S(2)}, u32[]{:S(2)}) collective-permute-start(bf16[256,512]{1,0:T(8,128)(2,1)S(1)} %constant_dynamic-update-slice_fusion.refs_0_), channel_id=1, source_target_pairs={{0,96},{32,0},{64,32},{96,64},{1,97},{33,1},{65,33},{97,65},{2,98}... | collective-permute-start | bytes 786440 | tf_op jit(solution)/shard_map/ppermute | solution.py:237
  22.7 12.8 %collective-permute-start.12 = (bf16[264,512]{1,0:T(8,128)(2,1)S(1)}, bf16[264,512]{1,0:T(8,128)(2,1)S(1)}, u32[]{:S(2)}, u32[]{:S(2)}) collective-permute-start(bf16[264,512]{1,0:T(8,128)(2,1)S(1)} %collective-permute-done.11.refs_5_), channel_id=1, source_target_pairs={{0,2},{2,4},{4,6},{6,8},{8,10},{10,12},{12,14},{14,0},{16,30},{18,... | collective-permute-start | bytes 811016 | tf_op jit(solution)/shard_map/ppermute | solution.py:32
  22.7 11.7 %collective-permute-start.2 = (bf16[256,512]{1,0:T(8,128)(2,1)S(1)}, bf16[256,512]{1,0:T(8,128)(2,1)S(1)}, u32[]{:S(2)}, u32[]{:S(2)}) collective-permute-start(bf16[256,512]{1,0:T(8,128)(2,1)S(1)} %constant_dynamic-update-slice_fusion.refs_0_), channel_id=1, source_target_pairs={{0,64},{32,96},{64,0},{96,32},{1,65},{33,97},{65,1},{97,33},{2,66}... | collective-permute-start | bytes 786440 | tf_op jit(solution)/shard_map/ppermute | solution.py:237
  24.8 14.3 %collective-permute-start.18 = (bf16[264,512]{1,0:T(8,128)(2,1)S(1)}, bf16[264,512]{1,0:T(8,128)(2,1)S(1)}, u32[]{:S(2)}, u32[]{:S(2)}) collective-permute-start(bf16[264,512]{1,0:T(8,128)(2,1)S(1)} %collective-permute-done.5.refs_4_), channel_id=1, source_target_pairs={{0,16},{16,0},{1,17},{17,1},{2,18},{18,2},{3,19},{19,3},{4,20},{20... | collective-permute-start | bytes 811016 | tf_op jit(solution)/shard_map/ppermute | solution.py:20
  27.5 11.6 %collective-permute-start.7 = (bf16[264,512]{1,0:T(8,128)(2,1)S(1)}, bf16[264,512]{1,0:T(8,128)(2,1)S(1)}, u32[]{:S(2)}, u32[]{:S(2)}) collective-permute-start(bf16[264,512]{1,0:T(8,128)(2,1)S(1)} %collective-permute-done.6.refs_4_), channel_id=1, source_target_pairs={{0,2},{2,4},{4,6},{6,8},{8,10},{10,12},{12,14},{14,0},{16,30},{18,... | collective-permute-start | bytes 811016 | tf_op jit(solution)/shard_map/ppermute | solution.py:32
  27.9 9.4 %collective-permute-start.3 = (bf16[256,512]{1,0:T(8,128)(2,1)S(1)}, bf16[256,512]{1,0:T(8,128)(2,1)S(1)}, u32[]{:S(2)}, u32[]{:S(2)}) collective-permute-start(bf16[256,512]{1,0:T(8,128)(2,1)S(1)} %constant_dynamic-update-slice_fusion.refs_0_), channel_id=1, source_target_pairs={{0,32},{32,64},{64,96},{96,0},{1,33},{33,65},{65,97},{97,1},{2,34}... | collective-permute-start | bytes 786440 | tf_op jit(solution)/shard_map/ppermute | solution.py:237
  34.4 10.4 %collective-permute-start.19 = (bf16[264,512]{1,0:T(8,128)(2,1)S(1)}, bf16[264,512]{1,0:T(8,128)(2,1)S(1)}, u32[]{:S(2)}, u32[]{:S(2)}) collective-permute-start(bf16[264,512]{1,0:T(8,128)(2,1)S(1)} %collective-permute-done.11.refs_5_), channel_id=1, source_target_pairs={{0,16},{16,0},{1,17},{17,1},{2,18},{18,2},{3,19},{19,3},{4,20},{20... | collective-permute-start | bytes 811016 | tf_op jit(solution)/shard_map/ppermute | solution.py:20
  35.5 9.4 %collective-permute-start.13 = (bf16[264,512]{1,0:T(8,128)(2,1)S(1)}, bf16[264,512]{1,0:T(8,128)(2,1)S(1)}, u32[]{:S(2)}, u32[]{:S(2)}) collective-permute-start(bf16[264,512]{1,0:T(8,128)(2,1)S(1)} %collective-permute-done.12.refs_5_), channel_id=1, source_target_pairs={{0,2},{2,4},{4,6},{6,8},{8,10},{10,12},{12,14},{14,0},{16,30},{18,... | collective-permute-start | bytes 811016 | tf_op jit(solution)/shard_map/ppermute | solution.py:32
  37.3 11.3 %collective-permute-start.16 = (bf16[264,512]{1,0:T(8,128)(2,1)S(1)}, bf16[264,512]{1,0:T(8,128)(2,1)S(1)}, u32[]{:S(2)}, u32[]{:S(2)}) collective-permute-start(bf16[264,512]{1,0:T(8,128)(2,1)S(1)} %collective-permute-done.6.refs_4_), channel_id=1, source_target_pairs={{0,16},{16,0},{1,17},{17,1},{2,18},{18,2},{3,19},{19,3},{4,20},{20... | collective-permute-start | bytes 811016 | tf_op jit(solution)/shard_map/ppermute | solution.py:20
  39.1 9.5 %collective-permute-start.17 = (bf16[264,512]{1,0:T(8,128)(2,1)S(1)}, bf16[264,512]{1,0:T(8,128)(2,1)S(1)}, u32[]{:S(2)}, u32[]{:S(2)}) collective-permute-start(bf16[264,512]{1,0:T(8,128)(2,1)S(1)} %collective-permute-done.12.refs_5_), channel_id=1, source_target_pairs={{0,16},{16,0},{1,17},{17,1},{2,18},{18,2},{3,19},{19,3},{4,20},{20... | collective-permute-start | bytes 811016 | tf_op jit(solution)/shard_map/ppermute | solution.py:20
  39.1 9.3 %collective-permute-start.8 = (bf16[264,512]{1,0:T(8,128)(2,1)S(1)}, bf16[264,512]{1,0:T(8,128)(2,1)S(1)}, u32[]{:S(2)}, u32[]{:S(2)}) collective-permute-start(bf16[264,512]{1,0:T(8,128)(2,1)S(1)} %collective-permute-done.7.refs_4_), channel_id=1, source_target_pairs={{0,2},{2,4},{4,6},{6,8},{8,10},{10,12},{12,14},{14,0},{16,30},{18,... | collective-permute-start | bytes 811016 | tf_op jit(solution)/shard_map/ppermute | solution.py:32
  44.8 6.9 %collective-permute-start.14 = (bf16[264,512]{1,0:T(8,128)(2,1)S(1)}, bf16[264,512]{1,0:T(8,128)(2,1)S(1)}, u32[]{:S(2)}, u32[]{:S(2)}) collective-permute-start(bf16[264,512]{1,0:T(8,128)(2,1)S(1)} %collective-permute-done.7.refs_4_), channel_id=1, source_target_pairs={{0,16},{16,0},{1,17},{17,1},{2,18},{18,2},{3,19},{19,3},{4,20},{20... | collective-permute-start | bytes 811016 | tf_op jit(solution)/shard_map/ppermute | solution.py:20
  44.9 6.8 %collective-permute-start.15 = (bf16[264,512]{1,0:T(8,128)(2,1)S(1)}, bf16[264,512]{1,0:T(8,128)(2,1)S(1)}, u32[]{:S(2)}, u32[]{:S(2)}) collective-permute-start(bf16[264,512]{1,0:T(8,128)(2,1)S(1)} %collective-permute-done.13.refs_5_), channel_id=1, source_target_pairs={{0,16},{16,0},{1,17},{17,1},{2,18},{18,2},{3,19},{19,3},{4,20},{20... | collective-permute-start | bytes 811016 | tf_op jit(solution)/shard_map/ppermute | solution.py:20
  48.4 7.8 %collective-permute-start.9 = (bf16[264,512]{1,0:T(8,128)(2,1)S(1)}, bf16[264,512]{1,0:T(8,128)(2,1)S(1)}, u32[]{:S(2)}, u32[]{:S(2)}) collective-permute-start(bf16[264,512]{1,0:T(8,128)(2,1)S(1)} %collective-permute-done.8.refs_4_), channel_id=1, source_target_pairs={{0,16},{16,0},{1,17},{17,1},{2,18},{18,2},{3,19},{19,3},{4,20},{20... | collective-permute-start | bytes 811016 | tf_op jit(solution)/shard_map/ppermute | solution.py:20
  57.1 9.3 %collective-permute-start.21 = (f32[2,128,512]{2,1,0:T(8,128)S(1)}, f32[2,128,512]{2,1,0:T(8,128)S(1)}, u32[]{:S(2)}, u32[]{:S(2)}) collective-permute-start(f32[2,128,512]{2,1,0:T(8,128)S(1)} %pad_maximum_fusion.1), channel_id=1, source_target_pairs={{0,1},{1,0},{16,145},{17,144},{128,129},{129,128},{144,17},{145,16... | collective-permute-start | bytes 1572872 | tf_op jit(solution)/shard_map/ppermute | solution.py:41
  57.8 14.2 %collective-permute-start.20 = (f32[2,128,512]{2,1,0:T(8,128)S(1)}, f32[2,128,512]{2,1,0:T(8,128)S(1)}, u32[]{:S(2)}, u32[]{:S(2)}) collective-permute-start(f32[2,128,512]{2,1,0:T(8,128)S(1)} %pad_maximum_fusion), channel_id=1, source_target_pairs={{0,1},{1,0},{16,145},{17,144},{128,129},{129,128},{144,17},{145,16... | collective-permute-start | bytes 1572872 | tf_op jit(solution)/shard_map/ppermute | solution.py:41
  66.4 11.5 %collective-permute-start.22 = (f32[128,512]{1,0:T(8,128)S(1)}, f32[128,512]{1,0:T(8,128)S(1)}, u32[]{:S(2)}, u32[]{:S(2)}) collective-permute-start(f32[128,512]{1,0:T(8,128)S(1)} %get-tuple-element.38), channel_id=1, source_target_pairs={{0,64},{32,96},{64,0},{96,32},{1,65},{33,97},{65,1},{97,33},{2,66}... | collective-permute-start | bytes 786440 | tf_op jit(solution)/shard_map/ppermute | solution.py:223
  70.9 12.4 %collective-permute-start.23 = (f32[128,512]{1,0:T(8,128)S(1)}, f32[128,512]{1,0:T(8,128)S(1)}, u32[]{:S(2)}, u32[]{:S(2)}) collective-permute-start(f32[128,512]{1,0:T(8,128)S(1)} %get-tuple-element.39), channel_id=1, source_target_pairs={{0,32},{32,64},{64,96},{96,0},{1,33},{33,65},{65,97},{97,1},{2,34}... | collective-permute-start | bytes 786440 | tf_op jit(solution)/shard_map/ppermute | solution.py:223
  72.0 11.5 %collective-permute-start.24 = (f32[128,512]{1,0:T(8,128)S(1)}, f32[128,512]{1,0:T(8,128)S(1)}, u32[]{:S(2)}, u32[]{:S(2)}) collective-permute-start(f32[128,512]{1,0:T(8,128)S(1)} %fusion.1), channel_id=1, source_target_pairs={{0,96},{32,0},{64,32},{96,64},{1,97},{33,1},{65,33},{97,65},{2,98}... | collective-permute-start | bytes 786440 | tf_op jit(solution)/shard_map/ppermute | solution.py:223
  83.6 53.3 %copy-start.3 = (bf16[128,512]{1,0:T(8,128)(2,1)}, bf16[128,512]{1,0:T(8,128)(2,1)S(1)}, u32[]{:S(2)}) copy-start(bf16[128,512]{1,0:T(8,128)(2,1)S(1)} %fusion.9) | copy-start | bytes 393220
  83.6 1.4 %collective-permute-start.25 = (bf16[128,512]{1,0:T(8,128)(2,1)S(1)}, bf16[128,512]{1,0:T(8,128)(2,1)S(1)}, u32[]{:S(2)}, u32[]{:S(2)}) collective-permute-start(bf16[128,512]{1,0:T(8,128)(2,1)S(1)} %fusion.9), channel_id=1, source_target_pairs={{0,16},{16,0},{1,17},{17,1},{2,18},{18,2},{3,19},{19,3},{4,20},{20... | collective-permute-start | bytes 393224 | tf_op jit(solution)/shard_map/ppermute | solution.py:20
  85.3 53.4 %copy-start.1 = (bf16[128,512]{1,0:T(8,128)(2,1)S(1)}, bf16[128,512]{1,0:T(8,128)(2,1)}, u32[]{:S(2)}) copy-start(bf16[128,512]{1,0:T(8,128)(2,1)} %features_ref.3) | copy-start | bytes 393220
  137.1 1.6 %collective-permute-start.26 = (bf16[256,512]{1,0:T(8,128)(2,1)S(1)}, bf16[256,512]{1,0:T(8,128)(2,1)S(1)}, u32[]{:S(2)}, u32[]{:S(2)}) collective-permute-start(bf16[256,512]{1,0:T(8,128)(2,1)S(1)} %reshape.15.own_ref), channel_id=1, source_target_pairs={{0,16},{16,0},{1,17},{17,1},{2,18},{18,2},{3,19},{19,3},{4,20},{20... | collective-permute-start | bytes 786440 | tf_op jit(solution)/shard_map/ppermute | solution.py:20

commit v2 on v1

--- a/solution.py
+++ b/solution.py
@@ -116,8 +116,7 @@
         store(other_ref, own_ref)
 
 
-def tile_kernel(first, sides, row_refs_count, chunk_count, *refs):
-    last = len(sides) == 1
+def tile_kernel(first, last, sides, row_refs_count, chunk_count, *refs):
     row_refs, refs = refs[:row_refs_count], refs[row_refs_count:]
     chunk_refs, refs = refs[:chunk_count], refs[chunk_count:]
     if not first:
@@ -174,15 +173,16 @@
             totals_ref[here, :] = totals
 
 
-def add_tiles(rows, chunks, carried, sides=(0, 1)):
+def add_tiles(rows, chunks, carried, sides=(0, 1), last=False):
     width = rows[0].shape[1]
-    row_count = sum(r.shape[0] for r in rows) * len(sides) // 2
+    row_count = sum(r.shape[0] for r in rows)
     columns = sum(chunk.shape[0] - EXTRA for chunk in chunks)
-    first, last = carried is None, len(sides) == 1
+    first = carried is None
     operands = [*rows, *chunks] + ([] if first else list(carried))
     aliases = {}
     if last:
-        out_shape = [jax.ShapeDtypeStruct((row_count // len(rows), width), F32)] * len(rows)
+        shard = row_count // len(rows) // 2
+        out_shape = [jax.ShapeDtypeStruct((shard, width), F32)] * len(rows)
     else:
         out_shape = [
             jax.ShapeDtypeStruct((row_count, width), F32),
@@ -191,8 +191,10 @@
         if not first:
             aliases = {len(operands) - 2: 0, len(operands) - 1: 1}
 
+    done = row_count * len(sides) // 2
+
     def body(*refs):
-        tile_kernel(first, sides, len(rows), len(chunks), *refs)
+        tile_kernel(first, last, sides, len(rows), len(chunks), *refs)
 
     return in_vmem(
         body,
@@ -201,27 +203,30 @@
         scratch_shapes=[pltpu.VMEM((columns, width), BF16)],
         input_output_aliases=aliases,
         cost_estimate=pl.CostEstimate(
-            flops=4 * row_count * columns * width,
-            bytes_accessed=4 * row_count * width,
-            transcendentals=row_count * columns,
+            flops=4 * done * columns * width,
+            bytes_accessed=4 * done * width,
+            transcendentals=done * columns,
         ),
     )
 
 
 def summed_partials(own, beside):
     count = len(own)
-    totals = [None] * count
-    parts = []
-    for at in ((2, 1), (3, 0)):
-        parts.append((at, beside_y(jnp.stack([beside[k] for k in at]))))
-    for at, part in parts:
-        for i, k in enumerate(at):
-            totals[k] = own[k] + part[i]
-    result = totals[0]
-    for k in (2, 1, 3):
-        pairs = [(x, (x + k) % count) for x in range(count)]
-        result = result + lax.ppermute(totals[k], "x", pairs)
-    return result
+    onward = [(x, (x + 1) % count) for x in range(count)]
+    back = [(x, (x - 1) % count) for x in range(count)]
+    half = own[0].shape[0] // 2
+    far = beside_y(beside[2])
+    sides = beside_y(jnp.stack([beside[1], beside[3]]))
+    near = beside_y(beside[0])
+    far = own[2] + far
+    up = lax.ppermute(far[:half], "x", onward)
+    down = lax.ppermute(far[half:], "x", back)
+    sums = [own[1] + sides[0], own[3] + sides[1]]
+    sums[0] = sums[0] + jnp.pad(up, ((0, half), (0, 0)))
+    sums[1] = sums[1] + jnp.pad(down, ((half, 0), (0, 0)))
+    from_below = lax.ppermute(sums[0], "x", onward)
+    from_above = lax.ppermute(sums[1], "x", back)
+    return own[0] + near + from_below + from_above
 
 
 def step(features, coefs):
@@ -249,11 +254,11 @@
         other_far = swapped(far, "c")
         groups.append([near, far, other_near, other_far])
 
-    carried = None
-    for group in groups[:-1]:
-        carried = add_tiles(rows, group, carried)
-    beside = add_tiles(rows, groups[-1], carried, sides=(1,))
-    own = add_tiles(rows, groups[-1], carried, sides=(0,))
+    carried, waiting = None, groups[-3] + groups[-2] + groups[-1]
+    for at, group in enumerate(groups[:-2]):
+        carried = add_tiles(rows, group, carried, (1,) if at == hops - 1 else (0, 1))
+    beside = add_tiles(rows, groups[-2] + groups[-1], carried, (1,), last=True)
+    own = add_tiles(rows, waiting, carried, (0,), last=True)
     grads = (2.0 * gamma * summed_partials(own, beside)).astype(BF16)
 
     core = lax.axis_index("c")
@@ -262,7 +267,9 @@
     own_half = jnp.where(core == 0, both[:, :half], both[:, half:])
     gram = jnp.einsum("pa,pb->ab", own_half, both, preferred_element_type=F32)
     chips = lax.axis_size(chip_axes)
-    parts = lax.all_to_all(gram.reshape(chips, -1, 128), chip_axes, 0, 0, tiled=True)
+    parts = lax.all_to_all(
+        gram.astype(BF16).reshape(chips, -1, LANES), chip_axes, 0, 0, tiled=True
+    ).astype(F32)
     point_count = points * chips * lax.axis_size("c")
     own_agop = (jnp.sum(parts, axis=0) / point_count).astype(BF16)
     own_rows = from_everyone(own_agop, chip_axes).reshape(half, width)

time: 142 us -> 132 us (0.930)
  blocking collectives: 51.4 us -> 44.8 us
  starting transfers between devices: 36.2 us -> 33.9 us
    all_to_all x1, blocking collectives: 30.7 us -> 24.8 us  [step(): lax.all_to_all(gram.astype(BF16).reshape(chips, -1, LANES), chip_axes, 0,...]
    ppermute x3 -> x4, waiting for transfers between devices: 6.38 us -> 1.5 us  [beside_y(): return lax.ppermute(value, ('yh', 'c', 'yl'), pairs)]
    ppermute x3 -> x4, waiting for transfers between devices: 7.55 us -> 12.1 us  [the longest x1 5.98 us: summed_partials(): from_below = lax.ppermute(sums[0], 'x', onward)]
    ppermute x3 -> x4, starting transfers between devices: 9.3 us -> 6.28 us  [the longest x1 2.57 us: summed_partials(): up = lax.ppermute(far[:half], 'x', onward)]
    pallas_call x10 -> x9, Pallas kernels: 14.8 us -> 14 us  [in_vmem(): pl.pallas_call(body, out_shape=out_shape, in_specs=[spec] * len(operands)...]
    ppermute x3 -> x4, starting transfers between devices: 3.78 us -> 4.55 us  [beside_y(): return lax.ppermute(value, ('yh', 'c', 'yl'), pairs)]
  transfers between devices with their start and end apart: 27 -> 29, of which waited for: 14 -> 14; matrix products, arithmetic and copies ran while one was open for 1% -> 1% of each run, Pallas kernels for 9% -> 9%
where the time goes in v2:
time: 132 us; the launch traced here: 130 us
  blocking collectives  44.8 us (34%)
  starting transfers between devices  33.9 us (26%)
  waiting for transfers between devices  32.7 us (25%)
  Pallas kernels  14 us (11%)
  local copies, waits for them, and re-layouts  2.88 us (2%)
    all_to_all x1, blocking collectives, step(): lax.all_to_all(gram.astype(BF16).reshape(chips, -1, LANES), chip_axes, 0,...  24.8 us
    all_to_all x1, blocking collectives, from_everyone(): return lax.all_to_all(copies, axes, split_axis=0, concat_axis=0, tiled=True)  19.9 us
    pallas_call x9, Pallas kernels, in_vmem(): pl.pallas_call(body, out_shape=out_shape, in_specs=[spec] * len(operands)...  14 us
    ppermute x11, starting transfers between devices, swapped(): return lax.ppermute(value, axis, [(0, 1), (1, 0)])  9.71 us
    ppermute x7, starting transfers between devices, along_z(): return lax.ppermute(value, ('c', 'z'), pairs)  9.12 us
    ppermute x11, waiting for transfers between devices, swapped(): return lax.ppermute(value, axis, [(0, 1), (1, 0)])  6.59 us
    ppermute x7, waiting for transfers between devices, along_z(): return lax.ppermute(value, ('c', 'z'), pairs)  6.37 us
    ppermute x3, waiting for transfers between devices, step(): rows.append(lax.ppermute(rows[0], 'x', pairs))  6.11 us
  transfers between devices with their start and end apart: 29, of which 14 were waited for; matrix products, arithmetic and copies ran while one was open for 1% of the time, Pallas kernels for 9%

profile of v2, /device:TPU:2, one launch (start us, length us, event | category | flops | bytes accessed | tf_op | source)
XLA Modules:
  0.0 129.7 jit_solution(14219021293801446342)
XLA Ops:
  0.6 0.0 copy-start
  0.6 0.9 copy-done
  1.5 0.7 copy-done.2
  2.2 0.2 shard_map.41.near_ref
  2.4 3.2 %collective-permute-start.4 = (bf16[136,512]{1,0:T(8,128)(2,1)S(1)}, bf16[136,512]{1,0:T(8,128)(2,1)S(1)}, u32[]{:S(2)}, u32[]{:S(2)}) collective-permute-start(bf16[136,512]{1,0:T(8,128)(2,1)S(1)} %shard_map.41.near_ref), channel_id=1, source_target_pairs={{0,128},{128,0},{1,129},{129,1},{2,130},{130,2},{3,131},{131,3},{4... | collective-permute-start | bytes 417800 | tf_op jit(solution)/shard_map/ppermute | solution.py:20
  5.6 3.7 %collective-permute-done.4.other_ref = bf16[136,512]{1,0:T(8,128)(2,1)S(1)} collective-permute-done((bf16[136,512]{1,0:T(8,128)(2,1)S(1)}, bf16[136,512]{1,0:T(8,128)(2,1)S(1)}, u32[]{:S(2)}, u32[]{:S(2)}) %collective-permute-start.4) | collective-permute-done | bytes 139296 | tf_op jit(solution)/shard_map/ppermute | solution.py:20
  9.4 0.1 collective-permute-start.8
  9.5 2.0 %collective-permute-start.5 = (bf16[264,512]{1,0:T(8,128)(2,1)S(1)}, bf16[264,512]{1,0:T(8,128)(2,1)S(1)}, u32[]{:S(2)}, u32[]{:S(2)}) collective-permute-start(bf16[264,512]{1,0:T(8,128)(2,1)S(1)} %shard_map.42.refs_4_), channel_id=1, source_target_pairs={{0,2},{2,4},{4,6},{6,8},{8,10},{10,12},{12,14},{14,0},{16,30},{18,... | collective-permute-start | bytes 811016 | tf_op jit(solution)/shard_map/ppermute | solution.py:32
  11.4 1.6 %collective-permute-start = (bf16[128,512]{1,0:T(8,128)(2,1)}, bf16[128,512]{1,0:T(8,128)(2,1)S(1)}, u32[]{:S(2)}, u32[]{:S(2)}) collective-permute-start(bf16[128,512]{1,0:T(8,128)(2,1)} %features_ref.3), channel_id=1, source_target_pairs={{0,1},{1,0},{16,145},{17,144},{128,129},{129,128},{144,17},{145,16... | collective-permute-start | bytes 393224 | tf_op jit(solution)/shard_map/ppermute | solution.py:41
  13.0 1.9 %collective-permute-start.9 = (bf16[264,512]{1,0:T(8,128)(2,1)S(1)}, bf16[264,512]{1,0:T(8,128)(2,1)S(1)}, u32[]{:S(2)}, u32[]{:S(2)}) collective-permute-start(bf16[264,512]{1,0:T(8,128)(2,1)S(1)} %collective-permute-done.8.refs_5_), channel_id=1, source_target_pairs={{0,2},{2,4},{4,6},{6,8},{8,10},{10,12},{12,14},{14,0},{16,30},{18,... | collective-permute-start | bytes 811016 | tf_op jit(solution)/shard_map/ppermute | solution.py:32
  14.9 0.9 constant_dynamic-update-slice_fusion.1
  15.9 4.0 %collective-permute-done.5.refs_4_ = bf16[264,512]{1,0:T(8,128)(2,1)S(1)} collective-permute-done((bf16[264,512]{1,0:T(8,128)(2,1)S(1)}, bf16[264,512]{1,0:T(8,128)(2,1)S(1)}, u32[]{:S(2)}, u32[]{:S(2)}) %collective-permute-start.5) | collective-permute-done | bytes 270368 | tf_op jit(solution)/shard_map/ppermute | solution.py:32
  19.8 0.0 collective-permute-start.6
  19.8 0.0 collective-permute-done
  19.8 0.6 collective-permute-start.1
  20.5 2.3 %collective-permute-done.9.refs_5_ = bf16[264,512]{1,0:T(8,128)(2,1)S(1)} collective-permute-done((bf16[264,512]{1,0:T(8,128)(2,1)S(1)}, bf16[264,512]{1,0:T(8,128)(2,1)S(1)}, u32[]{:S(2)}, u32[]{:S(2)}) %collective-permute-start.9) | collective-permute-done | bytes 270368 | tf_op jit(solution)/shard_map/ppermute | solution.py:32
  22.7 2.1 %collective-permute-start.2 = (bf16[256,512]{1,0:T(8,128)(2,1)S(1)}, bf16[256,512]{1,0:T(8,128)(2,1)S(1)}, u32[]{:S(2)}, u32[]{:S(2)}) collective-permute-start(bf16[256,512]{1,0:T(8,128)(2,1)S(1)} %constant_dynamic-update-slice_fusion.refs_0_), channel_id=1, source_target_pairs={{0,64},{32,96},{64,0},{96,32},{1,65},{33,97},{65,1},{97,33},{2,66}... | collective-permute-start | bytes 786440 | tf_op jit(solution)/shard_map/ppermute | solution.py:242
  24.8 2.5 %collective-permute-start.18 = (bf16[264,512]{1,0:T(8,128)(2,1)S(1)}, bf16[264,512]{1,0:T(8,128)(2,1)S(1)}, u32[]{:S(2)}, u32[]{:S(2)}) collective-permute-start(bf16[264,512]{1,0:T(8,128)(2,1)S(1)} %collective-permute-done.5.refs_4_), channel_id=1, source_target_pairs={{0,16},{16,0},{1,17},{17,1},{2,18},{18,2},{3,19},{19,3},{4,20},{20... | collective-permute-start | bytes 811016 | tf_op jit(solution)/shard_map/ppermute | solution.py:20
  27.4 0.1 collective-permute-done.6.refs_4_
  27.5 0.4 collective-permute-done.1.refs_1_
  27.9 1.5 %collective-permute-start.3 = (bf16[256,512]{1,0:T(8,128)(2,1)S(1)}, bf16[256,512]{1,0:T(8,128)(2,1)S(1)}, u32[]{:S(2)}, u32[]{:S(2)}) collective-permute-start(bf16[256,512]{1,0:T(8,128)(2,1)S(1)} %constant_dynamic-update-slice_fusion.refs_0_), channel_id=1, source_target_pairs={{0,32},{32,64},{64,96},{96,0},{1,33},{33,65},{65,97},{97,1},{2,34}... | collective-permute-start | bytes 786440 | tf_op jit(solution)/shard_map/ppermute | solution.py:242
  29.3 5.1 %collective-permute-done.2.refs_2_ = bf16[256,512]{1,0:T(8,128)(2,1)S(1)} collective-permute-done((bf16[256,512]{1,0:T(8,128)(2,1)S(1)}, bf16[256,512]{1,0:T(8,128)(2,1)S(1)}, u32[]{:S(2)}, u32[]{:S(2)}) %collective-permute-start.2) | collective-permute-done | bytes 262176 | tf_op jit(solution)/shard_map/ppermute | solution.py:242
  34.4 1.1 collective-permute-start.19
  35.5 1.1 collective-permute-start.11
  36.6 0.7 collective-permute-done.3.refs_3_
  37.3 1.8 %collective-permute-start.16 = (bf16[264,512]{1,0:T(8,128)(2,1)S(1)}, bf16[264,512]{1,0:T(8,128)(2,1)S(1)}, u32[]{:S(2)}, u32[]{:S(2)}) collective-permute-start(bf16[264,512]{1,0:T(8,128)(2,1)S(1)} %collective-permute-done.6.refs_4_), channel_id=1, source_target_pairs={{0,16},{16,0},{1,17},{17,1},{2,18},{18,2},{3,19},{19,3},{4,20},{20... | collective-permute-start | bytes 811016 | tf_op jit(solution)/shard_map/ppermute | solution.py:20
  39.1 0.0 collective-permute-start.17
  39.1 4.1 %collective-permute-start.14 = (bf16[264,512]{1,0:T(8,128)(2,1)S(1)}, bf16[264,512]{1,0:T(8,128)(2,1)S(1)}, u32[]{:S(2)}, u32[]{:S(2)}) collective-permute-start(bf16[264,512]{1,0:T(8,128)(2,1)S(1)} %collective-permute-done.7.refs_4_), channel_id=1, source_target_pairs={{0,2},{2,4},{4,6},{6,8},{8,10},{10,12},{12,14},{14,0},{16,30},{18,... | collective-permute-start | bytes 811016 | tf_op jit(solution)/shard_map/ppermute | solution.py:32
  43.2 1.6 %shard_map.43 = (f32[1024,512]{1,0:T(8,128)S(1)}, f32[1024,128]{1,0:T(8,128)S(1)}) custom-call(bf16[256,512]{1,0:T(8,128)(2,1)S(1)} %constant_dynamic-update-slice_fusion.refs_0_, bf16[256,512]{1,0:T(8,128)(2,1)S(1)} %collective-permute-done.1.refs_1_, bf16[256,512]{1,0:T(8,128)(2,1)S(1)} %collective-permute-done.2.refs_2_, ...), custom_call_target="tpu_custom_call" | custom-call | flops 1073741824 | bytes 2097152 | tf_op jit(solution)/shard_map/pallas_call | solution.py:47
  44.8 0.1 collective-permute-start.12
  44.9 0.5 collective-permute-start.13
  45.4 3.0 %shard_map.44 = (f32[1024,512]{1,0:T(8,128)S(1)}, f32[1024,128]{1,0:T(8,128)S(1)}) custom-call(bf16[256,512]{1,0:T(8,128)(2,1)S(1)} %constant_dynamic-update-slice_fusion.refs_0_, bf16[256,512]{1,0:T(8,128)(2,1)S(1)} %collective-permute-done.1.refs_1_, ...), custom_call_target="tpu_custom_call", output_to_operand_aliasing={{0}: (8, {}), {1}: (9, {})} | custom-call | flops 2147483648 | bytes 2097152 | tf_op jit(solution)/shard_map/pallas_call | solution.py:47
  48.4 0.2 collective-permute-start.15
  48.6 3.0 %shard_map.45 = (f32[1024,512]{1,0:T(8,128)S(1)}, f32[1024,128]{1,0:T(8,128)S(1)}) custom-call(bf16[256,512]{1,0:T(8,128)(2,1)S(1)} %constant_dynamic-update-slice_fusion.refs_0_, bf16[256,512]{1,0:T(8,128)(2,1)S(1)} %collective-permute-done.1.refs_1_, ...), custom_call_target="tpu_custom_call", output_to_operand_aliasing={{0}: (8, {}), {1}: (9, {})} | custom-call | flops 2147483648 | bytes 2097152 | tf_op jit(solution)/shard_map/pallas_call | solution.py:47
  51.7 1.8 %shard_map.46 = (f32[1024,512]{1,0:T(8,128)S(1)}, f32[1024,128]{1,0:T(8,128)S(1)}) custom-call(bf16[256,512]{1,0:T(8,128)(2,1)S(1)} %constant_dynamic-update-slice_fusion.refs_0_, bf16[256,512]{1,0:T(8,128)(2,1)S(1)} %collective-permute-done.1.refs_1_, ...), custom_call_target="tpu_custom_call", output_to_operand_aliasing={{0}: (8, {}), {1}: (9, {})} | custom-call | flops 1073741824 | bytes 1048576 | tf_op jit(solution)/shard_map/pallas_call | solution.py:47
  53.5 1.0 shard_map.48
  54.5 0.7 collective-permute-start.22
  55.2 1.8 %collective-permute-start.21 = (f32[2,128,512]{2,1,0:T(8,128)S(1)}, f32[2,128,512]{2,1,0:T(8,128)S(1)}, u32[]{:S(2)}, u32[]{:S(2)}) collective-permute-start(f32[2,128,512]{2,1,0:T(8,128)S(1)} %pad_maximum_fusion), channel_id=1, source_target_pairs={{0,1},{1,0},{16,145},{17,144},{128,129},{129,128},{144,17},{145,16... | collective-permute-start | bytes 1572872 | tf_op jit(solution)/shard_map/ppermute | solution.py:41
  57.0 2.5 %shard_map.47 = (f32[128,512]{1,0:T(8,128)S(1)}, f32[128,512]{1,0:T(8,128)S(1)}, f32[128,512]{1,0:T(8,128)S(1)}, f32[128,512]{1,0:T(8,128)S(1)}) custom-call(bf16[256,512]{1,0:T(8,128)(2,1)S(1)} %constant_dynamic-update-slice_fusion.refs_0_, bf16[256,512]{1,0:T(8,128)(2,1)S(1)} %collective-permute-done.1.refs_1_, ...), custom_call_target="tpu_custom_call" | custom-call | flops 1610612736 | bytes 1048576 | tf_op jit(solution)/shard_map/pallas_call | solution.py:47
  59.5 1.5 %collective-permute-done.22 = f32[128,512]{1,0:T(8,128)S(1)} collective-permute-done((f32[128,512]{1,0:T(8,128)S(1)}, f32[128,512]{1,0:T(8,128)S(1)}, u32[]{:S(2)}, u32[]{:S(2)}) %collective-permute-start.22) | collective-permute-done | bytes 262176 | tf_op jit(solution)/shard_map/ppermute | solution.py:41
  61.0 2.6 %collective-permute-start.23 = (f32[64,512]{1,0:T(8,128)S(1)}, f32[64,512]{1,0:T(8,128)S(1)}, u32[]{:S(2)}, u32[]{:S(2)}) collective-permute-start(f32[64,512]{1,0:T(8,128)S(1)} %get-tuple-element.36), channel_id=1, source_target_pairs={{0,32},{32,64},{64,96},{96,0},{1,33},{33,65},{65,97},{97,1},{2,34}... | collective-permute-start | bytes 393224 | tf_op jit(solution)/shard_map/ppermute | solution.py:222
  63.6 1.4 %collective-permute-start.25 = (f32[64,512]{1,0:T(8,128)S(1)}, f32[64,512]{1,0:T(8,128)S(1)}, u32[]{:S(2)}, u32[]{:S(2)}) collective-permute-start(f32[64,512]{1,0:T(8,128)S(1)} %get-tuple-element.37), channel_id=1, source_target_pairs={{0,96},{32,0},{64,32},{96,64},{1,97},{33,1},{65,33},{97,65},{2,98}... | collective-permute-start | bytes 393224 | tf_op jit(solution)/shard_map/ppermute | solution.py:223
  65.0 0.6 collective-permute-start.20
  65.6 3.5 %collective-permute-done.23 = f32[64,512]{1,0:T(8,128)S(1)} collective-permute-done((f32[64,512]{1,0:T(8,128)S(1)}, f32[64,512]{1,0:T(8,128)S(1)}, u32[]{:S(2)}, u32[]{:S(2)}) %collective-permute-start.23) | collective-permute-done | bytes 131104 | tf_op jit(solution)/shard_map/ppermute | solution.py:222
  69.1 0.9 collective-permute-done.25
  69.9 0.1 fusion.3
  70.0 1.8 %collective-permute-start.24 = (f32[128,512]{1,0:T(8,128)S(1)}, f32[128,512]{1,0:T(8,128)S(1)}, u32[]{:S(2)}, u32[]{:S(2)}) collective-permute-start(f32[128,512]{1,0:T(8,128)S(1)} %get-tuple-element.34), channel_id=1, source_target_pairs={{0,32},{32,64},{64,96},{96,0},{1,33},{33,65},{65,97},{97,1},{2,34}... | collective-permute-start | bytes 786440 | tf_op jit(solution)/shard_map/ppermute | solution.py:227
  71.9 0.4 collective-permute-start.26
  72.3 6.0 %collective-permute-done.24 = f32[128,512]{1,0:T(8,128)S(1)} collective-permute-done((f32[128,512]{1,0:T(8,128)S(1)}, f32[128,512]{1,0:T(8,128)S(1)}, u32[]{:S(2)}, u32[]{:S(2)}) %collective-permute-start.24) | collective-permute-done | bytes 262176 | tf_op jit(solution)/shard_map/ppermute | solution.py:227
  78.3 1.8 %collective-permute-done.26 = f32[128,512]{1,0:T(8,128)S(1)} collective-permute-done((f32[128,512]{1,0:T(8,128)S(1)}, f32[128,512]{1,0:T(8,128)S(1)}, u32[]{:S(2)}, u32[]{:S(2)}) %collective-permute-start.26) | collective-permute-done | bytes 262176 | tf_op jit(solution)/shard_map/ppermute | solution.py:228
  80.1 0.1 multiply_convert_fusion
  80.2 0.0 copy-start.3
  80.2 0.0 copy-start.1
  80.2 0.1 collective-permute-start.27
  80.3 1.3 %collective-permute-done.27 = bf16[128,512]{1,0:T(8,128)(2,1)S(1)} collective-permute-done((bf16[128,512]{1,0:T(8,128)(2,1)S(1)}, bf16[128,512]{1,0:T(8,128)(2,1)S(1)}, u32[]{:S(2)}, u32[]{:S(2)}) %collective-permute-start.27) | collective-permute-done | bytes 131104 | tf_op jit(solution)/shard_map/ppermute | solution.py:20
  81.6 0.3 convolution_convert_fusion
  81.9 0.2 reshape.14
  82.1 24.8 %all_to_all.10 = bf16[128,8,128]{2,1,0:T(8,128)(2,1)S(1)} all-to-all(bf16[128,8,128]{2,1,0:T(8,128)(2,1)S(1)} %reshape.14), channel_id=1, replica_groups=mesh['yh'=2,'x'=4,'c'=2,'z'=8,'yl'=2] {'yh','x','z','yl'}, dimensions={0} | all-to-all | bytes 524288 | tf_op jit(solution)/shard_map/all_to_all | solution.py:270
  106.9 0.1 convert_reduce_fusion
  107.1 19.9 %all_to_all.11 = bf16[128,8,128]{2,1,0:T(8,128)(2,1)S(1)} all-to-all(bf16[128,8,128]{2,1,0:T(8,128)(2,1)S(1)} %broadcast_in_dim.3), channel_id=1, replica_groups=mesh['yh'=2,'x'=4,'c'=2,'z'=8,'yl'=2] {'yh','x','z','yl'}, dimensions={0} | all-to-all | bytes 524288 | tf_op jit(solution)/shard_map/all_to_all | solution.py:25
  127.0 0.2 reshape.15.own_ref
  127.2 0.1 collective-permute-start.28
  127.3 1.5 %collective-permute-done.28.other_ref = bf16[256,512]{1,0:T(8,128)(2,1)S(1)} collective-permute-done((bf16[256,512]{1,0:T(8,128)(2,1)S(1)}, bf16[256,512]{1,0:T(8,128)(2,1)S(1)}, u32[]{:S(2)}, u32[]{:S(2)}) %collective-permute-start.28) | collective-permute-done | bytes 262176 | tf_op jit(solution)/shard_map/ppermute | solution.py:20
  128.8 0.9 shard_map.49
  (26 shorter events, 0.2 us)
Async XLA Ops:
  0.6 0.9 copy-start
  1.5 0.7 copy-start.2
  2.4 7.0 %collective-permute-start.4 = (bf16[136,512]{1,0:T(8,128)(2,1)S(1)}, bf16[136,512]{1,0:T(8,128)(2,1)S(1)}, u32[]{:S(2)}, u32[]{:S(2)}) collective-permute-start(bf16[136,512]{1,0:T(8,128)(2,1)S(1)} %shard_map.41.near_ref), channel_id=1, source_target_pairs={{0,128},{128,0},{1,129},{129,1},{2,130},{130,2},{3,131},{131,3},{4... | collective-permute-start | bytes 417800 | tf_op jit(solution)/shard_map/ppermute | solution.py:20
  9.4 3.7 %collective-permute-start.8 = (bf16[264,512]{1,0:T(8,128)(2,1)S(1)}, bf16[264,512]{1,0:T(8,128)(2,1)S(1)}, u32[]{:S(2)}, u32[]{:S(2)}) collective-permute-start(bf16[264,512]{1,0:T(8,128)(2,1)S(1)} %shard_map.42.refs_4_), channel_id=1, source_target_pairs={{0,16},{16,0},{1,17},{17,1},{2,18},{18,2},{3,19},{19,3},{4,20},{20... | collective-permute-start | bytes 811016 | tf_op jit(solution)/shard_map/ppermute | solution.py:20
  9.5 10.4 %collective-permute-start.5 = (bf16[264,512]{1,0:T(8,128)(2,1)S(1)}, bf16[264,512]{1,0:T(8,128)(2,1)S(1)}, u32[]{:S(2)}, u32[]{:S(2)}) collective-permute-start(bf16[264,512]{1,0:T(8,128)(2,1)S(1)} %shard_map.42.refs_4_), channel_id=1, source_target_pairs={{0,2},{2,4},{4,6},{6,8},{8,10},{10,12},{12,14},{14,0},{16,30},{18,... | collective-permute-start | bytes 811016 | tf_op jit(solution)/shard_map/ppermute | solution.py:32
  11.4 8.4 %collective-permute-start = (bf16[128,512]{1,0:T(8,128)(2,1)}, bf16[128,512]{1,0:T(8,128)(2,1)S(1)}, u32[]{:S(2)}, u32[]{:S(2)}) collective-permute-start(bf16[128,512]{1,0:T(8,128)(2,1)} %features_ref.3), channel_id=1, source_target_pairs={{0,1},{1,0},{16,145},{17,144},{128,129},{129,128},{144,17},{145,16... | collective-permute-start | bytes 393224 | tf_op jit(solution)/shard_map/ppermute | solution.py:41
  13.0 9.7 %collective-permute-start.9 = (bf16[264,512]{1,0:T(8,128)(2,1)S(1)}, bf16[264,512]{1,0:T(8,128)(2,1)S(1)}, u32[]{:S(2)}, u32[]{:S(2)}) collective-permute-start(bf16[264,512]{1,0:T(8,128)(2,1)S(1)} %collective-permute-done.8.refs_5_), channel_id=1, source_target_pairs={{0,2},{2,4},{4,6},{6,8},{8,10},{10,12},{12,14},{14,0},{16,30},{18,... | collective-permute-start | bytes 811016 | tf_op jit(solution)/shard_map/ppermute | solution.py:32
  19.8 7.7 %collective-permute-start.6 = (bf16[264,512]{1,0:T(8,128)(2,1)S(1)}, bf16[264,512]{1,0:T(8,128)(2,1)S(1)}, u32[]{:S(2)}, u32[]{:S(2)}) collective-permute-start(bf16[264,512]{1,0:T(8,128)(2,1)S(1)} %collective-permute-done.5.refs_4_), channel_id=1, source_target_pairs={{0,2},{2,4},{4,6},{6,8},{8,10},{10,12},{12,14},{14,0},{16,30},{18,... | collective-permute-start | bytes 811016 | tf_op jit(solution)/shard_map/ppermute | solution.py:32
  19.8 8.0 %collective-permute-start.1 = (bf16[256,512]{1,0:T(8,128)(2,1)S(1)}, bf16[256,512]{1,0:T(8,128)(2,1)S(1)}, u32[]{:S(2)}, u32[]{:S(2)}) collective-permute-start(bf16[256,512]{1,0:T(8,128)(2,1)S(1)} %constant_dynamic-update-slice_fusion.refs_0_), channel_id=1, source_target_pairs={{0,96},{32,0},{64,32},{96,64},{1,97},{33,1},{65,33},{97,65},{2,98}... | collective-permute-start | bytes 786440 | tf_op jit(solution)/shard_map/ppermute | solution.py:242
  22.7 12.8 %collective-permute-start.10 = (bf16[264,512]{1,0:T(8,128)(2,1)S(1)}, bf16[264,512]{1,0:T(8,128)(2,1)S(1)}, u32[]{:S(2)}, u32[]{:S(2)}) collective-permute-start(bf16[264,512]{1,0:T(8,128)(2,1)S(1)} %collective-permute-done.9.refs_5_), channel_id=1, source_target_pairs={{0,2},{2,4},{4,6},{6,8},{8,10},{10,12},{12,14},{14,0},{16,30},{18,... | collective-permute-start | bytes 811016 | tf_op jit(solution)/shard_map/ppermute | solution.py:32
  22.7 11.7 %collective-permute-start.2 = (bf16[256,512]{1,0:T(8,128)(2,1)S(1)}, bf16[256,512]{1,0:T(8,128)(2,1)S(1)}, u32[]{:S(2)}, u32[]{:S(2)}) collective-permute-start(bf16[256,512]{1,0:T(8,128)(2,1)S(1)} %constant_dynamic-update-slice_fusion.refs_0_), channel_id=1, source_target_pairs={{0,64},{32,96},{64,0},{96,32},{1,65},{33,97},{65,1},{97,33},{2,66}... | collective-permute-start | bytes 786440 | tf_op jit(solution)/shard_map/ppermute | solution.py:242
  24.8 14.3 %collective-permute-start.18 = (bf16[264,512]{1,0:T(8,128)(2,1)S(1)}, bf16[264,512]{1,0:T(8,128)(2,1)S(1)}, u32[]{:S(2)}, u32[]{:S(2)}) collective-permute-start(bf16[264,512]{1,0:T(8,128)(2,1)S(1)} %collective-permute-done.5.refs_4_), channel_id=1, source_target_pairs={{0,16},{16,0},{1,17},{17,1},{2,18},{18,2},{3,19},{19,3},{4,20},{20... | collective-permute-start | bytes 811016 | tf_op jit(solution)/shard_map/ppermute | solution.py:20
  27.5 11.6 %collective-permute-start.7 = (bf16[264,512]{1,0:T(8,128)(2,1)S(1)}, bf16[264,512]{1,0:T(8,128)(2,1)S(1)}, u32[]{:S(2)}, u32[]{:S(2)}) collective-permute-start(bf16[264,512]{1,0:T(8,128)(2,1)S(1)} %collective-permute-done.6.refs_4_), channel_id=1, source_target_pairs={{0,2},{2,4},{4,6},{6,8},{8,10},{10,12},{12,14},{14,0},{16,30},{18,... | collective-permute-start | bytes 811016 | tf_op jit(solution)/shard_map/ppermute | solution.py:32
  27.9 9.4 %collective-permute-start.3 = (bf16[256,512]{1,0:T(8,128)(2,1)S(1)}, bf16[256,512]{1,0:T(8,128)(2,1)S(1)}, u32[]{:S(2)}, u32[]{:S(2)}) collective-permute-start(bf16[256,512]{1,0:T(8,128)(2,1)S(1)} %constant_dynamic-update-slice_fusion.refs_0_), channel_id=1, source_target_pairs={{0,32},{32,64},{64,96},{96,0},{1,33},{33,65},{65,97},{97,1},{2,34}... | collective-permute-start | bytes 786440 | tf_op jit(solution)/shard_map/ppermute | solution.py:242
  34.4 10.4 %collective-permute-start.19 = (bf16[264,512]{1,0:T(8,128)(2,1)S(1)}, bf16[264,512]{1,0:T(8,128)(2,1)S(1)}, u32[]{:S(2)}, u32[]{:S(2)}) collective-permute-start(bf16[264,512]{1,0:T(8,128)(2,1)S(1)} %collective-permute-done.9.refs_5_), channel_id=1, source_target_pairs={{0,16},{16,0},{1,17},{17,1},{2,18},{18,2},{3,19},{19,3},{4,20},{20... | collective-permute-start | bytes 811016 | tf_op jit(solution)/shard_map/ppermute | solution.py:20
  35.5 9.4 %collective-permute-start.11 = (bf16[264,512]{1,0:T(8,128)(2,1)S(1)}, bf16[264,512]{1,0:T(8,128)(2,1)S(1)}, u32[]{:S(2)}, u32[]{:S(2)}) collective-permute-start(bf16[264,512]{1,0:T(8,128)(2,1)S(1)} %collective-permute-done.10.refs_5_), channel_id=1, source_target_pairs={{0,2},{2,4},{4,6},{6,8},{8,10},{10,12},{12,14},{14,0},{16,30},{18,... | collective-permute-start | bytes 811016 | tf_op jit(solution)/shard_map/ppermute | solution.py:32
  37.3 11.3 %collective-permute-start.16 = (bf16[264,512]{1,0:T(8,128)(2,1)S(1)}, bf16[264,512]{1,0:T(8,128)(2,1)S(1)}, u32[]{:S(2)}, u32[]{:S(2)}) collective-permute-start(bf16[264,512]{1,0:T(8,128)(2,1)S(1)} %collective-permute-done.6.refs_4_), channel_id=1, source_target_pairs={{0,16},{16,0},{1,17},{17,1},{2,18},{18,2},{3,19},{19,3},{4,20},{20... | collective-permute-start | bytes 811016 | tf_op jit(solution)/shard_map/ppermute | solution.py:20
  39.1 9.5 %collective-permute-start.17 = (bf16[264,512]{1,0:T(8,128)(2,1)S(1)}, bf16[264,512]{1,0:T(8,128)(2,1)S(1)}, u32[]{:S(2)}, u32[]{:S(2)}) collective-permute-start(bf16[264,512]{1,0:T(8,128)(2,1)S(1)} %collective-permute-done.10.refs_5_), channel_id=1, source_target_pairs={{0,16},{16,0},{1,17},{17,1},{2,18},{18,2},{3,19},{19,3},{4,20},{20... | collective-permute-start | bytes 811016 | tf_op jit(solution)/shard_map/ppermute | solution.py:20
  39.1 9.3 %collective-permute-start.14 = (bf16[264,512]{1,0:T(8,128)(2,1)S(1)}, bf16[264,512]{1,0:T(8,128)(2,1)S(1)}, u32[]{:S(2)}, u32[]{:S(2)}) collective-permute-start(bf16[264,512]{1,0:T(8,128)(2,1)S(1)} %collective-permute-done.7.refs_4_), channel_id=1, source_target_pairs={{0,2},{2,4},{4,6},{6,8},{8,10},{10,12},{12,14},{14,0},{16,30},{18,... | collective-permute-start | bytes 811016 | tf_op jit(solution)/shard_map/ppermute | solution.py:32
  44.8 6.9 %collective-permute-start.12 = (bf16[264,512]{1,0:T(8,128)(2,1)S(1)}, bf16[264,512]{1,0:T(8,128)(2,1)S(1)}, u32[]{:S(2)}, u32[]{:S(2)}) collective-permute-start(bf16[264,512]{1,0:T(8,128)(2,1)S(1)} %collective-permute-done.7.refs_4_), channel_id=1, source_target_pairs={{0,16},{16,0},{1,17},{17,1},{2,18},{18,2},{3,19},{19,3},{4,20},{20... | collective-permute-start | bytes 811016 | tf_op jit(solution)/shard_map/ppermute | solution.py:20
  44.9 6.8 %collective-permute-start.13 = (bf16[264,512]{1,0:T(8,128)(2,1)S(1)}, bf16[264,512]{1,0:T(8,128)(2,1)S(1)}, u32[]{:S(2)}, u32[]{:S(2)}) collective-permute-start(bf16[264,512]{1,0:T(8,128)(2,1)S(1)} %collective-permute-done.11.refs_5_), channel_id=1, source_target_pairs={{0,16},{16,0},{1,17},{17,1},{2,18},{18,2},{3,19},{19,3},{4,20},{20... | collective-permute-start | bytes 811016 | tf_op jit(solution)/shard_map/ppermute | solution.py:20
  48.4 5.0 %collective-permute-start.15 = (bf16[264,512]{1,0:T(8,128)(2,1)S(1)}, bf16[264,512]{1,0:T(8,128)(2,1)S(1)}, u32[]{:S(2)}, u32[]{:S(2)}) collective-permute-start(bf16[264,512]{1,0:T(8,128)(2,1)S(1)} %collective-permute-done.14.refs_8_.refs_4_), channel_id=1, source_target_pairs={{0,16},{16,0},{1,17},{17,1},{2,18},{18,2},{3,19},{19,3},{4,20},{20... | collective-permute-start | bytes 811016 | tf_op jit(solution)/shard_map/ppermute | solution.py:20
  54.5 6.5 %collective-permute-start.22 = (f32[128,512]{1,0:T(8,128)S(1)}, f32[128,512]{1,0:T(8,128)S(1)}, u32[]{:S(2)}, u32[]{:S(2)}) collective-permute-start(f32[128,512]{1,0:T(8,128)S(1)} %get-tuple-element.32), channel_id=1, source_target_pairs={{0,1},{1,0},{16,145},{17,144},{128,129},{129,128},{144,17},{145,16... | collective-permute-start | bytes 786440 | tf_op jit(solution)/shard_map/ppermute | solution.py:41
  55.2 14.7 %collective-permute-start.21 = (f32[2,128,512]{2,1,0:T(8,128)S(1)}, f32[2,128,512]{2,1,0:T(8,128)S(1)}, u32[]{:S(2)}, u32[]{:S(2)}) collective-permute-start(f32[2,128,512]{2,1,0:T(8,128)S(1)} %pad_maximum_fusion), channel_id=1, source_target_pairs={{0,1},{1,0},{16,145},{17,144},{128,129},{129,128},{144,17},{145,16... | collective-permute-start | bytes 1572872 | tf_op jit(solution)/shard_map/ppermute | solution.py:41
  61.0 8.0 %collective-permute-start.23 = (f32[64,512]{1,0:T(8,128)S(1)}, f32[64,512]{1,0:T(8,128)S(1)}, u32[]{:S(2)}, u32[]{:S(2)}) collective-permute-start(f32[64,512]{1,0:T(8,128)S(1)} %get-tuple-element.36), channel_id=1, source_target_pairs={{0,32},{32,64},{64,96},{96,0},{1,33},{33,65},{65,97},{97,1},{2,34}... | collective-permute-start | bytes 393224 | tf_op jit(solution)/shard_map/ppermute | solution.py:222
  63.6 6.3 %collective-permute-start.25 = (f32[64,512]{1,0:T(8,128)S(1)}, f32[64,512]{1,0:T(8,128)S(1)}, u32[]{:S(2)}, u32[]{:S(2)}) collective-permute-start(f32[64,512]{1,0:T(8,128)S(1)} %get-tuple-element.37), channel_id=1, source_target_pairs={{0,96},{32,0},{64,32},{96,64},{1,97},{33,1},{65,33},{97,65},{2,98}... | collective-permute-start | bytes 393224 | tf_op jit(solution)/shard_map/ppermute | solution.py:223
  65.0 7.3 %collective-permute-start.20 = (f32[128,512]{1,0:T(8,128)S(1)}, f32[128,512]{1,0:T(8,128)S(1)}, u32[]{:S(2)}, u32[]{:S(2)}) collective-permute-start(f32[128,512]{1,0:T(8,128)S(1)} %get-tuple-element.27), channel_id=1, source_target_pairs={{0,1},{1,0},{16,145},{17,144},{128,129},{129,128},{144,17},{145,16... | collective-permute-start | bytes 786440 | tf_op jit(solution)/shard_map/ppermute | solution.py:41
  70.0 8.3 %collective-permute-start.24 = (f32[128,512]{1,0:T(8,128)S(1)}, f32[128,512]{1,0:T(8,128)S(1)}, u32[]{:S(2)}, u32[]{:S(2)}) collective-permute-start(f32[128,512]{1,0:T(8,128)S(1)} %get-tuple-element.34), channel_id=1, source_target_pairs={{0,32},{32,64},{64,96},{96,0},{1,33},{33,65},{65,97},{97,1},{2,34}... | collective-permute-start | bytes 786440 | tf_op jit(solution)/shard_map/ppermute | solution.py:227
  71.9 8.2 %collective-permute-start.26 = (f32[128,512]{1,0:T(8,128)S(1)}, f32[128,512]{1,0:T(8,128)S(1)}, u32[]{:S(2)}, u32[]{:S(2)}) collective-permute-start(f32[128,512]{1,0:T(8,128)S(1)} %get-tuple-element.35), channel_id=1, source_target_pairs={{0,96},{32,0},{64,32},{96,64},{1,97},{33,1},{65,33},{97,65},{2,98}... | collective-permute-start | bytes 786440 | tf_op jit(solution)/shard_map/ppermute | solution.py:228
  80.2 49.5 %copy-start.3 = (bf16[128,512]{1,0:T(8,128)(2,1)}, bf16[128,512]{1,0:T(8,128)(2,1)S(1)}, u32[]{:S(2)}) copy-start(bf16[128,512]{1,0:T(8,128)(2,1)S(1)} %multiply_convert_fusion) | copy-start | bytes 393220
  80.2 48.6 %copy-start.1 = (bf16[128,512]{1,0:T(8,128)(2,1)S(1)}, bf16[128,512]{1,0:T(8,128)(2,1)}, u32[]{:S(2)}) copy-start(bf16[128,512]{1,0:T(8,128)(2,1)} %features_ref.3) | copy-start | bytes 393220
  80.2 1.4 %collective-permute-start.27 = (bf16[128,512]{1,0:T(8,128)(2,1)S(1)}, bf16[128,512]{1,0:T(8,128)(2,1)S(1)}, u32[]{:S(2)}, u32[]{:S(2)}) collective-permute-start(bf16[128,512]{1,0:T(8,128)(2,1)S(1)} %multiply_convert_fusion), channel_id=1, source_target_pairs={{0,16},{16,0},{1,17},{17,1},{2,18},{18,2},{3,19},{19,3},{4,20},{20... | collective-permute-start | bytes 393224 | tf_op jit(solution)/shard_map/ppermute | solution.py:20
  127.2 1.6 %collective-permute-start.28 = (bf16[256,512]{1,0:T(8,128)(2,1)S(1)}, bf16[256,512]{1,0:T(8,128)(2,1)S(1)}, u32[]{:S(2)}, u32[]{:S(2)}) collective-permute-start(bf16[256,512]{1,0:T(8,128)(2,1)S(1)} %reshape.15.own_ref), channel_id=1, source_target_pairs={{0,16},{16,0},{1,17},{17,1},{2,18},{18,2},{3,19},{19,3},{4,20},{20... | collective-permute-start | bytes 786440 | tf_op jit(solution)/shard_map/ppermute | solution.py:20
